TPU v7x, 32 devices: a whole 2x2x4 slice. The times are simulated.
32 devices in a mesh: leaf: 8 (over z, y), top: 4 (over x, core).
Axes of the slice: x: 2, y: 2, z: 4, core: 2. Of those that a mesh axis runs over, the one named last changes fastest.
Arguments:
- charges: float32 [4, 16, 4096], P('top', None, 'leaf'), may hold values from -6 to 6
- leaf_basis: float32 [4, 64, 64, 64], P('top', 'leaf'), may hold values from -0.75 to 0.75
- near_blocks: float32 [4, 64, 3, 64, 64], P('top', 'leaf'), may hold values from -0.4375 to 0.4375
- near_list: int32 [4, 64, 3], P('top', 'leaf'), may hold values from 0 to 8
- local_transfer: float32 [4, 112, 64, 64], P('top', 'leaf'), may hold values from -0.5 to 0.5
- local_coupling: float32 [4, 112, 3, 64, 64], P('top', 'leaf'), may hold values from -0.4375 to 0.4375
- coupling_list: int32 [4, 112, 3], P('top', 'leaf'), may hold values from 0 to 23, as said below
- coarse_transfer: float32 [4, 3, 2, 64, 64], P('top'), may hold values from -0.5 to 0.5
- coarse_coupling: float32 [4, 1, 4, 64, 64], P('top'), may hold values from -0.4375 to 0.4375
- opposite_coupling: float32 [4, 64, 64], P('top'), may hold values from -0.75 to 0.75
- body_coupling: float32 [4, 3, 64, 64], P('top'), may hold values from -0.4375 to 0.4375
Outputs:
- potential: float32 [4, 16, 4096], P('top', None, 'leaf')
Inputs may be any that keep to these rules, and one draw needn't show every extreme that they name: `coupling_list`: for a node of a device tier with m nodes per device the entry lies below 3 m; it names, in order, the m nodes of that tier on the previous device along the boundary, then this device's, then the next device's.
All inputs are finite; a program needn't handle non-finite values.
Results may differ from a plain program's by a relative error of at most 0.0001.
Values sent between devices are 32-bit elements; how exact they have to be, the bound alone decides.
No kernel may reach another device: no remote copies, remote signals or barrier semaphores. Data moves between devices by JAX's collectives and lax.ppermute only.
A program may use at most 64 MiB of HBM per device.

v0:
```python
import jax
import jax.numpy as jnp
from jax import lax
from jax.sharding import PartitionSpec as P

NEAR = 4


HIGH = lax.Precision.HIGHEST
OFFSETS = (-3, -2, 2, 3)


def padded_2(block, sides, width):
    for axis, dim in sides:
        count = lax.axis_size(axis)
        forward = [(i, i + 1) for i in range(count - 1)]
        forward.append((count - 1, 0))
        backward = [(target, source) for source, target in forward]
        low = lax.ppermute(
            lax.slice_in_dim(block, block.shape[dim] - width, None, axis=dim), axis, forward
        )
        high = lax.ppermute(lax.slice_in_dim(block, 0, width, axis=dim), axis, backward)
        block = jnp.concatenate([low, block, high], axis=dim)
    return block


def from_partner(block, axis, stride):
    count = lax.axis_size(axis)
    route = []
    for low in range(count):
        high = low | 1 << stride
        if high != low and high < count:
            route += [(low, high), (high, low)]
    return lax.ppermute(block, axis, route)


def from_behind(shard, axis, by):
    count = lax.axis_size(axis)
    return lax.ppermute(shard, axis, [(i, (i + by) % count) for i in range(count)])


def times_matrix(coeff, matrix):
    return jnp.einsum("rnk,kj->rnj", coeff, matrix, precision=HIGH)


def times_transposed(coeff, matrix):
    return jnp.einsum("rnj,kj->rnk", coeff, matrix, precision=HIGH)


def per_device(
    charges,
    leaf_basis,
    near_blocks,
    near_list,
    local_transfer,
    local_coupling,
    coupling_list,
    coarse_transfer,
    coarse_coupling,
    opposite_coupling,
    body_coupling,
):
    density = charges[0]
    basis = leaf_basis[0]
    leaves_here = basis.shape[0]
    points = basis.shape[1]
    rhs = density.shape[0]
    levels_here = leaves_here.bit_length() - 1
    coarse = lax.axis_size("leaf").bit_length() - 1
    position = lax.axis_index("leaf")
    transfer = local_transfer[0]
    coupling = local_coupling[0]
    lists = coupling_list[0]
    up_mats = coarse_transfer[0]
    couple_mats = coarse_coupling[0]
    opposite = opposite_coupling[0]
    padded = padded_2(density, (("leaf", 1),), NEAR * points)
    blocks = density.reshape(rhs, leaves_here, points)
    coeffs = [jnp.einsum("rnp,npk->rnk", blocks, basis, precision=HIGH)]
    for height in range(levels_here):
        members = leaves_here >> height
        first = 2 * leaves_here - 2 * members
        moved = jnp.einsum(
            "rnk,nkj->rnj", coeffs[-1], transfer[first : first + members], precision=HIGH
        )
        coeffs.append(moved[:, 0::2] + moved[:, 1::2])
    device_coeff = coeffs[-1]
    tiers = [device_coeff]
    for height in range(coarse):
        side = position >> height & 1
        matrix = jnp.where(side == 0, up_mats[height, 0], up_mats[height, 1])
        term = times_matrix(tiers[-1], matrix)
        tiers.append(term + from_partner(term, "leaf", height))
    top_coeff = tiers[-1]
    bodies = lax.all_gather(top_coeff, "top", axis=1, tiled=True)
    here = lax.axis_index("top")
    many = lax.axis_size("top")
    body_local = jnp.zeros_like(top_coeff)
    for which in range(many - 1):
        source = lax.dynamic_slice_in_dim(bodies, (here + 1 + which) % many, 1, 1)
        body_local = body_local + times_matrix(source, body_coupling[0, which])
    local = body_local
    for height in range(coarse - 1, -1, -1):
        tier = tiers[height]
        parity = position >> height & 1
        if height <= coarse - 3:
            offsets = OFFSETS
        elif height == coarse - 2:
            offsets = (2,)
        else:
            offsets = ()
        coupled = jnp.zeros_like(tier)
        for which, offset in enumerate(offsets):
            distant = from_behind(tier, "leaf", -offset * (1 << height))
            if height <= coarse - 3:
                matrix = couple_mats[height, which]
            else:
                matrix = opposite
            moved = times_matrix(distant, matrix)
            if offset == -3:
                keep = parity == 1
            elif offset == 3:
                keep = parity == 0
            else:
                keep = parity >= 0
            coupled = coupled + jnp.where(keep, moved, 0.0)
        matrix = jnp.where(parity == 0, up_mats[height, 0], up_mats[height, 1])
        local = coupled + times_transposed(local, matrix)
    device_local = local
    nodes = 2 * leaves_here - 2
    stacked = jnp.concatenate(coeffs[:levels_here], axis=1)
    widened = padded_2(stacked, (("leaf", 1),), nodes)
    widened = widened.reshape(rhs, 3, nodes, widened.shape[2])
    local = device_local
    for height in range(levels_here - 1, -1, -1):
        members = leaves_here >> height
        first = 2 * leaves_here - 2 * members
        window = widened[:, :, first : first + members].reshape(rhs, 3 * members, widened.shape[3])
        picked = window[:, lists[first : first + members]]
        coupled = jnp.einsum(
            "rnsk,nskj->rnj", picked, coupling[first : first + members], precision=HIGH
        )
        parent = jnp.repeat(local, 2, axis=1)
        down = jnp.einsum("rnj,nkj->rnk", parent, transfer[first : first + members], precision=HIGH)
        local = coupled + down
    far = jnp.einsum("rnk,npk->rnp", local, basis, precision=HIGH)
    wide_blocks = padded.reshape(rhs, leaves_here + 2 * NEAR, points)
    source = jnp.arange(leaves_here, dtype=jnp.int32)[:, None] + near_list[0]
    gathered = wide_blocks[:, source]
    near = jnp.einsum("rnsq,nsqp->rnp", gathered, near_blocks[0], precision=HIGH)
    return (far + near).reshape(1, rhs, leaves_here * points)


def solution(mesh):
    in_specs = (
        P("top", None, "leaf"),
        P("top", "leaf", None, None),
        P("top", "leaf", None, None, None),
        P("top", "leaf", None),
        P("top", "leaf", None, None),
        P("top", "leaf", None, None, None),
        P("top", "leaf", None),
        P("top", None, None, None, None),
        P("top", None, None, None, None),
        P("top", None, None),
        P("top", None, None, None),
    )
    out_specs = P("top", None, "leaf")
    return jax.shard_map(
        per_device, mesh=mesh, in_specs=in_specs, out_specs=out_specs, check_vma=False
    )
```

profile of v0, /device:TPU:0, one launch (start us, length us, event | category | flops | bytes accessed | tf_op | source)
XLA Modules:
  0.0 51.3 jit_solution(17709632666760907653)
XLA Ops:
  0.1 0.9 %reshape_squeeze.3 = f32[16,8,64]{2,1,0:T(8,128)S(1)} reshape(f32[1,16,512]{2,1,0:T(8,128)} %param.11) | data formatting | bytes 65536 | tf_op jit(solution)/shard_map/reshape;squeeze | solution.py:78
  1.0 1.3 %convolution_bitcast_fusion.3 = f32[16,8,64]{2,0,1:T(8,128)S(1)} fusion(f32[1,8,64,64]{3,2,1,0:T(8,128)} %param.12, f32[16,8,64]{2,1,0:T(8,128)S(1)} %reshape_squeeze.3), kind=kOutput, calls=%fused_computation.11 | convolution fusion | flops 6291456 | bytes 196608 | tf_op jit(solution)/shard_map/rnp,npk->rnk/dot_general | solution.py:79
  2.3 1.3 %convolution_bitcast_fusion.2 = f32[16,8,64]{2,0,1:T(8,128)S(1)} fusion(f32[16,8,64]{2,0,1:T(8,128)S(1)} %convolution_bitcast_fusion.3, f32[1,14,64,64]{3,2,1,0:T(8,128)} %param.15), kind=kOutput, calls=%fused_computation.10 | convolution fusion | flops 6291456 | bytes 327680 | tf_op jit(solution)/shard_map/rnk,nkj->rnj/dot_general | solution.py:83
  3.6 1.1 %convolution_bitcast_fusion.4 = f32[16,4,64]{2,0,1:T(8,128)S(1)} fusion(f32[16,4,64]{2,0,1:T(8,128)S(1)} %slice_add_fusion, f32[1,14,64,64]{3,2,1,0:T(8,128)} %param.15), kind=kOutput, calls=%fused_computation.14 | convolution fusion | flops 3145728 | bytes 163840 | tf_op jit(solution)/shard_map/rnk,nkj->rnj/dot_general | solution.py:83
  4.7 1.0 %convolution_bitcast_fusion.6 = f32[16,2,64]{2,0,1:T(8,128)S(1)} fusion(f32[16,2,64]{2,0,1:T(8,128)S(1)} %slice_add_fusion.1, f32[1,14,64,64]{3,2,1,0:T(8,128)} %param.15), kind=kOutput, calls=%fused_computation.18 | convolution fusion | flops 1572864 | bytes 81920 | tf_op jit(solution)/shard_map/rnk,nkj->rnj/dot_general | solution.py:83
  5.7 5.1 %collective-permute-start.5 = (f32[16,1,64]{2,0,1:T(8,128)S(1)}, f32[16,1,64]{2,0,1:T(8,128)S(1)}, u32[]{:S(2)}, u32[]{:S(2)}) collective-permute-start(f32[16,1,64]{2,0,1:T(8,128)S(1)} %slice_add_fusion.2), channel_id=1, source_target_pairs={{0,20},{4,24},{8,28},{12,0},{16,4},{20,8},{24,12},{28,16},{1,21},{... | collective-permute-start | bytes 12296 | tf_op jit(solution)/shard_map/ppermute | solution.py:39
  10.8 1.3 %collective-permute-start.4 = (f32[16,1,64]{2,0,1:T(8,128)S(1)}, f32[16,1,64]{2,0,1:T(8,128)S(1)}, u32[]{:S(2)}, u32[]{:S(2)}) collective-permute-start(f32[16,1,64]{2,0,1:T(8,128)S(1)} %slice_add_fusion.2), channel_id=1, source_target_pairs={{0,24},{4,28},{8,0},{12,4},{16,8},{20,12},{24,16},{28,20},{1,25},{... | collective-permute-start | bytes 12296 | tf_op jit(solution)/shard_map/ppermute | solution.py:39
  12.1 0.7 %collective-permute-start.3 = (f32[16,1,64]{2,0,1:T(8,128)S(1)}, f32[16,1,64]{2,0,1:T(8,128)S(1)}, u32[]{:S(2)}, u32[]{:S(2)}) collective-permute-start(f32[16,1,64]{2,0,1:T(8,128)S(1)} %slice_add_fusion.2), channel_id=1, source_target_pairs={{0,8},{4,12},{8,16},{12,20},{16,24},{20,28},{24,0},{28,4},{1,9},{5... | collective-permute-start | bytes 12296 | tf_op jit(solution)/shard_map/ppermute | solution.py:39
  12.8 1.0 %collective-permute-start.2 = (f32[16,1,64]{2,0,1:T(8,128)S(1)}, f32[16,1,64]{2,0,1:T(8,128)S(1)}, u32[]{:S(2)}, u32[]{:S(2)}) collective-permute-start(f32[16,1,64]{2,0,1:T(8,128)S(1)} %slice_add_fusion.2), channel_id=1, source_target_pairs={{0,12},{4,16},{8,20},{12,24},{16,28},{20,0},{24,4},{28,8},{1,13},{... | collective-permute-start | bytes 12296 | tf_op jit(solution)/shard_map/ppermute | solution.py:39
  13.9 1.5 %collective-permute-start.6 = (f32[16,1,64]{2,0,1:T(8,128)S(1)}, f32[16,1,64]{2,0,1:T(8,128)S(1)}, u32[]{:S(2)}, u32[]{:S(2)}) collective-permute-start(f32[16,1,64]{2,0,1:T(8,128)S(1)} %convolution_bitcast_fusion.10), channel_id=1, source_target_pairs={{0,4},{4,0},{8,12},{12,8},{16,20},{20,16},{24,28},{28,24},{1,5},{5... | collective-permute-start | bytes 12296 | tf_op jit(solution)/shard_map/ppermute | solution.py:34
  16.4 1.2 %collective-permute-done.6 = f32[16,1,64]{2,0,1:T(8,128)S(1)} collective-permute-done((f32[16,1,64]{2,0,1:T(8,128)S(1)}, f32[16,1,64]{2,0,1:T(8,128)S(1)}, u32[]{:S(2)}, u32[]{:S(2)}) %collective-permute-start.6) | collective-permute-done | bytes 4128 | tf_op jit(solution)/shard_map/ppermute | solution.py:34
  17.6 1.5 %collective-permute-start = (f32[16,14,64]{2,0,1:T(8,128)S(1)}, f32[16,14,64]{2,0,1:T(8,128)S(1)}, u32[]{:S(2)}, u32[]{:S(2)}) collective-permute-start(f32[16,14,64]{2,0,1:T(8,128)S(1)} %pad_maximum_fusion), channel_id=1, source_target_pairs={{0,4},{4,8},{8,12},{12,16},{16,20},{20,24},{24,28},{28,0},{1,5},{5... | collective-permute-start | bytes 172040 | tf_op jit(solution)/shard_map/ppermute | solution.py:19
  19.1 3.2 %collective-permute-start.1 = (f32[16,14,64]{2,0,1:T(8,128)S(1)}, f32[16,14,64]{2,0,1:T(8,128)S(1)}, u32[]{:S(2)}, u32[]{:S(2)}) collective-permute-start(f32[16,14,64]{2,0,1:T(8,128)S(1)} %pad_maximum_fusion), channel_id=1, source_target_pairs={{4,0},{8,4},{12,8},{16,12},{20,16},{24,20},{28,24},{0,28},{5,1},{9... | collective-permute-start | bytes 172040 | tf_op jit(solution)/shard_map/ppermute | solution.py:22
  23.2 3.1 %collective-permute-done.8 = f32[16,1,64]{2,0,1:T(8,128)S(1)} collective-permute-done((f32[16,1,64]{2,0,1:T(8,128)S(1)}, f32[16,1,64]{2,0,1:T(8,128)S(1)}, u32[]{:S(2)}, u32[]{:S(2)}) %collective-permute-start.8) | collective-permute-done | bytes 4128 | tf_op jit(solution)/shard_map/ppermute | solution.py:34
  26.5 1.6 %collective-permute-start.9 = (f32[16,1,64]{2,0,1:T(8,128)S(1)}, f32[16,1,64]{2,0,1:T(8,128)S(1)}, u32[]{:S(2)}, u32[]{:S(2)}) collective-permute-start(f32[16,1,64]{2,0,1:T(8,128)S(1)} %convolution_bitcast_fusion.8), channel_id=1, source_target_pairs={{0,16},{16,0},{4,20},{20,4},{8,24},{24,8},{12,28},{28,12},{1,17},{... | collective-permute-start | bytes 12296 | tf_op jit(solution)/shard_map/ppermute | solution.py:34
  28.2 2.9 %collective-permute-done.9 = f32[16,1,64]{2,0,1:T(8,128)S(1)} collective-permute-done((f32[16,1,64]{2,0,1:T(8,128)S(1)}, f32[16,1,64]{2,0,1:T(8,128)S(1)}, u32[]{:S(2)}, u32[]{:S(2)}) %collective-permute-start.9) | collective-permute-done | bytes 4128 | tf_op jit(solution)/shard_map/ppermute | solution.py:34
  31.1 1.5 %collective-permute-start.7 = (f32[16,1,64]{2,0,1:T(8,128)S(1)}, f32[16,1,64]{2,0,1:T(8,128)S(1)}, u32[]{:S(2)}, u32[]{:S(2)}) collective-permute-start(f32[16,1,64]{2,0,1:T(8,128)S(1)} %add.168), channel_id=1, source_target_pairs={{0,16},{4,20},{8,24},{12,28},{16,0},{20,4},{24,8},{28,12},{1,17},{... | collective-permute-start | bytes 12296 | tf_op jit(solution)/shard_map/ppermute | solution.py:39
  32.6 5.2 %all_gather.3 = f32[16,4,64]{2,0,1:T(8,128)S(1)} all-gather(f32[16,1,64]{2,0,1:T(8,128)S(1)} %add.170), channel_id=1, replica_groups=mesh['leaf'=8,'top'=4] {'top'}, dimensions={1}, use_global_device_ids=true | all-gather | bytes 20480 | tf_op jit(solution)/shard_map/all_gather | solution.py:95
  38.6 3.9 %collective-permute-start.11 = (f32[16,256]{1,0:T(8,128)S(1)}, f32[16,256]{1,0:T(8,128)S(1)}, u32[]{:S(2)}, u32[]{:S(2)}) collective-permute-start(f32[16,256]{1,0:T(8,128)S(1)} %get-tuple-element.6), channel_id=1, source_target_pairs={{4,0},{8,4},{12,8},{16,12},{20,16},{24,20},{28,24},{0,28},{5,1},{9... | collective-permute-start | bytes 49160 | tf_op jit(solution)/shard_map/ppermute | solution.py:22
  43.0 0.9 %collective-permute-done.11 = f32[16,256]{1,0:T(8,128)S(1)} collective-permute-done((f32[16,256]{1,0:T(8,128)S(1)}, f32[16,256]{1,0:T(8,128)S(1)}, u32[]{:S(2)}, u32[]{:S(2)}) %collective-permute-start.11) | collective-permute-done | bytes 16416 | tf_op jit(solution)/shard_map/ppermute | solution.py:22
  47.8 0.6 %gather_fusion = f32[24,16,64]{2,1,0:T(8,128)S(1)} fusion(f32[16,24,64]{2,0,1:T(8,128)S(1)} %bitcast.195, s32[1024]{0:T(1024)S(1)} %get-tuple-element.10), kind=kCustom, calls=%fused_computation | custom fusion | bytes 196704 | tf_op jit(solution)/shard_map/gather | solution.py:139
  48.4 0.8 %fusion.3 = f32[16,8,64]{2,0,1:T(8,128)S(1)} fusion(f32[8,16,64]{2,1,0:T(8,128)S(1)} %fusion.16, f32[16,8,3,64]{3,0,2,1:T(8,128)S(1)} %bitcast.197, f32[1,14,3,64,64]{4,3,2,1,0:T(8,128)S(1)} %copy-done.2), kind=kOutput, calls=%fused_computation.9 | convolution fusion | flops 18882560 | bytes 1081344 | tf_op jit(solution)/shard_map/rnsk,nskj->rnj/dot_general | solution.py:140
  49.7 0.8 %fusion.1 = f32[16,8,64]{2,0,1:T(8,128)S(1)} fusion(f32[8,16,64]{2,1,0:T(8,128)S(1)} %fusion.19, f32[16,8,3,64]{3,0,2,1:T(8,128)S(1)} %bitcast.196, f32[1,8,3,64,64]{4,3,2,1,0:T(8,128)S(1)} %copy-done), kind=kOutput, calls=%fused_computation.6 | convolution fusion | flops 18882560 | bytes 557056 | tf_op jit(solution)/shard_map/rnsq,nsqp->rnp/dot_general | solution.py:150
  50.6 0.7 %reshape.238 = f32[1,16,512]{2,1,0:T(8,128)} reshape(f32[16,8,64]{2,1,0:T(8,128)S(1)} %copy.39) | data formatting | bytes 65536 | tf_op jit(solution)/shard_map/reshape | solution.py:151
  (91 shorter events, 7.8 us)
Async XLA Ops:
  0.0 49.7 %copy-start = (f32[1,8,3,64,64]{4,3,2,1,0:T(8,128)S(1)}, f32[1,8,3,64,64]{4,3,2,1,0:T(8,128)}, u32[]{:S(2)}) copy-start(f32[1,8,3,64,64]{4,3,2,1,0:T(8,128)} %param.13) | copy-start | bytes 1179652
  0.0 16.3 %copy-start.4 = (f32[1,16,512]{2,1,0:T(8,128)S(1)}, f32[1,16,512]{2,1,0:T(8,128)}, u32[]{:S(2)}) copy-start(f32[1,16,512]{2,1,0:T(8,128)} %param.11) | copy-start | bytes 98308
  0.0 13.8 %copy-start.5 = (f32[1,3,2,64,64]{4,3,2,1,0:T(8,128)S(1)}, f32[1,3,2,64,64]{4,3,2,1,0:T(8,128)}, u32[]{:S(2)}) copy-start(f32[1,3,2,64,64]{4,3,2,1,0:T(8,128)} %param.18) | copy-start | bytes 294916
  0.0 15.5 %copy-start.9 = (s32[1,14,3]{1,0,2:T(1,128)S(1)}, s32[1,14,3]{1,0,2:T(1,128)}, u32[]{:S(2)}) copy-start(s32[1,14,3]{1,0,2:T(1,128)} %param.17) | copy-start | bytes 508
  0.0 15.6 %copy-start.10 = (s32[1,8,3]{1,0,2:T(1,128)S(1)}, s32[1,8,3]{1,0,2:T(1,128)}, u32[]{:S(2)}) copy-start(s32[1,8,3]{1,0,2:T(1,128)} %param.14) | copy-start | bytes 292
  0.0 22.3 %copy-start.6 = (f32[1,1,4,64,64]{4,3,2,1,0:T(8,128)S(1)}, f32[1,1,4,64,64]{4,3,2,1,0:T(8,128)}, u32[]{:S(2)}) copy-start(f32[1,1,4,64,64]{4,3,2,1,0:T(8,128)} %param.19) | copy-start | bytes 196612
  0.0 37.8 %copy-start.7 = (f32[1,3,64,64]{3,2,1,0:T(8,128)S(1)}, f32[1,3,64,64]{3,2,1,0:T(8,128)}, u32[]{:S(2)}) copy-start(f32[1,3,64,64]{3,2,1,0:T(8,128)} %param.21) | copy-start | bytes 147460
  0.0 42.4 %copy-start.8 = (f32[1,64,64]{2,1,0:T(8,128)S(1)}, f32[1,64,64]{2,1,0:T(8,128)}, u32[]{:S(2)}) copy-start(f32[1,64,64]{2,1,0:T(8,128)} %param.20) | copy-start | bytes 49156
  5.7 13.4 %collective-permute-start.5 = (f32[16,1,64]{2,0,1:T(8,128)S(1)}, f32[16,1,64]{2,0,1:T(8,128)S(1)}, u32[]{:S(2)}, u32[]{:S(2)}) collective-permute-start(f32[16,1,64]{2,0,1:T(8,128)S(1)} %slice_add_fusion.2), channel_id=1, source_target_pairs={{0,20},{4,24},{8,28},{12,0},{16,4},{20,8},{24,12},{28,16},{1,21},{... | collective-permute-start | bytes 12296 | tf_op jit(solution)/shard_map/ppermute | solution.py:39
  10.8 11.8 %collective-permute-start.4 = (f32[16,1,64]{2,0,1:T(8,128)S(1)}, f32[16,1,64]{2,0,1:T(8,128)S(1)}, u32[]{:S(2)}, u32[]{:S(2)}) collective-permute-start(f32[16,1,64]{2,0,1:T(8,128)S(1)} %slice_add_fusion.2), channel_id=1, source_target_pairs={{0,24},{4,28},{8,0},{12,4},{16,8},{20,12},{24,16},{28,20},{1,25},{... | collective-permute-start | bytes 12296 | tf_op jit(solution)/shard_map/ppermute | solution.py:39
  12.1 14.4 %collective-permute-start.3 = (f32[16,1,64]{2,0,1:T(8,128)S(1)}, f32[16,1,64]{2,0,1:T(8,128)S(1)}, u32[]{:S(2)}, u32[]{:S(2)}) collective-permute-start(f32[16,1,64]{2,0,1:T(8,128)S(1)} %slice_add_fusion.2), channel_id=1, source_target_pairs={{0,8},{4,12},{8,16},{12,20},{16,24},{20,28},{24,0},{28,4},{1,9},{5... | collective-permute-start | bytes 12296 | tf_op jit(solution)/shard_map/ppermute | solution.py:39
  12.8 30.0 %collective-permute-start.2 = (f32[16,1,64]{2,0,1:T(8,128)S(1)}, f32[16,1,64]{2,0,1:T(8,128)S(1)}, u32[]{:S(2)}, u32[]{:S(2)}) collective-permute-start(f32[16,1,64]{2,0,1:T(8,128)S(1)} %slice_add_fusion.2), channel_id=1, source_target_pairs={{0,12},{4,16},{8,20},{12,24},{16,28},{20,0},{24,4},{28,8},{1,13},{... | collective-permute-start | bytes 12296 | tf_op jit(solution)/shard_map/ppermute | solution.py:39
  13.9 3.7 %collective-permute-start.6 = (f32[16,1,64]{2,0,1:T(8,128)S(1)}, f32[16,1,64]{2,0,1:T(8,128)S(1)}, u32[]{:S(2)}, u32[]{:S(2)}) collective-permute-start(f32[16,1,64]{2,0,1:T(8,128)S(1)} %convolution_bitcast_fusion.10), channel_id=1, source_target_pairs={{0,4},{4,0},{8,12},{12,8},{16,20},{20,16},{24,28},{28,24},{1,5},{5... | collective-permute-start | bytes 12296 | tf_op jit(solution)/shard_map/ppermute | solution.py:34
  17.6 27.1 %collective-permute-start = (f32[16,14,64]{2,0,1:T(8,128)S(1)}, f32[16,14,64]{2,0,1:T(8,128)S(1)}, u32[]{:S(2)}, u32[]{:S(2)}) collective-permute-start(f32[16,14,64]{2,0,1:T(8,128)S(1)} %pad_maximum_fusion), channel_id=1, source_target_pairs={{0,4},{4,8},{8,12},{12,16},{16,20},{20,24},{24,28},{28,0},{1,5},{5... | collective-permute-start | bytes 172040 | tf_op jit(solution)/shard_map/ppermute | solution.py:19
  19.1 25.6 %collective-permute-start.1 = (f32[16,14,64]{2,0,1:T(8,128)S(1)}, f32[16,14,64]{2,0,1:T(8,128)S(1)}, u32[]{:S(2)}, u32[]{:S(2)}) collective-permute-start(f32[16,14,64]{2,0,1:T(8,128)S(1)} %pad_maximum_fusion), channel_id=1, source_target_pairs={{4,0},{8,4},{12,8},{16,12},{20,16},{24,20},{28,24},{0,28},{5,1},{9... | collective-permute-start | bytes 172040 | tf_op jit(solution)/shard_map/ppermute | solution.py:22
  22.6 3.7 %collective-permute-start.8 = (f32[16,1,64]{2,0,1:T(8,128)S(1)}, f32[16,1,64]{2,0,1:T(8,128)S(1)}, u32[]{:S(2)}, u32[]{:S(2)}) collective-permute-start(f32[16,1,64]{2,0,1:T(8,128)S(1)} %convolution_bitcast_fusion.9), channel_id=1, source_target_pairs={{0,8},{8,0},{4,12},{12,4},{16,24},{24,16},{20,28},{28,20},{1,9},{9... | collective-permute-start | bytes 12296 | tf_op jit(solution)/shard_map/ppermute | solution.py:34
  26.4 16.6 %collective-permute-start.10 = (f32[16,256]{1,0:T(8,128)S(1)}, f32[16,256]{1,0:T(8,128)S(1)}, u32[]{:S(2)}, u32[]{:S(2)}) collective-permute-start(f32[16,256]{1,0:T(8,128)S(1)} %get-tuple-element.5), channel_id=1, source_target_pairs={{0,4},{4,8},{8,12},{12,16},{16,20},{20,24},{24,28},{28,0},{1,5},{5... | collective-permute-start | bytes 49160 | tf_op jit(solution)/shard_map/ppermute | solution.py:19
  26.5 4.6 %collective-permute-start.9 = (f32[16,1,64]{2,0,1:T(8,128)S(1)}, f32[16,1,64]{2,0,1:T(8,128)S(1)}, u32[]{:S(2)}, u32[]{:S(2)}) collective-permute-start(f32[16,1,64]{2,0,1:T(8,128)S(1)} %convolution_bitcast_fusion.8), channel_id=1, source_target_pairs={{0,16},{16,0},{4,20},{20,4},{8,24},{24,8},{12,28},{28,12},{1,17},{... | collective-permute-start | bytes 12296 | tf_op jit(solution)/shard_map/ppermute | solution.py:34
  31.1 7.5 %collective-permute-start.7 = (f32[16,1,64]{2,0,1:T(8,128)S(1)}, f32[16,1,64]{2,0,1:T(8,128)S(1)}, u32[]{:S(2)}, u32[]{:S(2)}) collective-permute-start(f32[16,1,64]{2,0,1:T(8,128)S(1)} %add.168), channel_id=1, source_target_pairs={{0,16},{4,20},{8,24},{12,28},{16,0},{20,4},{24,8},{28,12},{1,17},{... | collective-permute-start | bytes 12296 | tf_op jit(solution)/shard_map/ppermute | solution.py:39
  38.6 5.3 %collective-permute-start.11 = (f32[16,256]{1,0:T(8,128)S(1)}, f32[16,256]{1,0:T(8,128)S(1)}, u32[]{:S(2)}, u32[]{:S(2)}) collective-permute-start(f32[16,256]{1,0:T(8,128)S(1)} %get-tuple-element.6), channel_id=1, source_target_pairs={{4,0},{8,4},{12,8},{16,12},{20,16},{24,20},{28,24},{0,28},{5,1},{9... | collective-permute-start | bytes 49160 | tf_op jit(solution)/shard_map/ppermute | solution.py:22
  42.8 2.6 %copy-start.2 = (f32[1,14,3,64,64]{4,3,2,1,0:T(8,128)S(1)}, f32[1,14,3,64,64]{4,3,2,1,0:T(8,128)}, u32[]{:S(2)}) copy-start(f32[1,14,3,64,64]{4,3,2,1,0:T(8,128)} %param.16) | copy-start | bytes 2064388
  44.6 2.1 %copy-start.1 = (f32[1,14,64,64]{3,2,1,0:T(8,128)S(1)}, f32[1,14,64,64]{3,2,1,0:T(8,128)}, u32[]{:S(2)}) copy-start(f32[1,14,64,64]{3,2,1,0:T(8,128)} %param.15) | copy-start | bytes 688132
  46.7 2.5 %copy-start.3 = (f32[1,8,64,64]{3,2,1,0:T(8,128)S(1)}, f32[1,8,64,64]{3,2,1,0:T(8,128)}, u32[]{:S(2)}) copy-start(f32[1,8,64,64]{3,2,1,0:T(8,128)} %param.12) | copy-start | bytes 393220
where the time goes:
time: 51.5 us; the launch traced here: 51.3 us
  starting transfers between devices  21.7 us (42%)
  matrix products  10.6 us (21%)
  waiting for transfers between devices  8.2 us (16%)
  blocking collectives  5.17 us (10%)
  local copies, waits for them, and re-layouts  4.95 us (10%)
    ppermute x5, starting transfers between devices, from_behind(): lax.ppermute(shard, axis, [(i, (i + by) % count) for i in range(count)])  9.57 us
    ppermute x3, waiting for transfers between devices, from_partner(): return lax.ppermute(block, axis, route)  7.2 us
    ppermute x2, starting transfers between devices, padded_2(): lax.ppermute(lax.slice_in_dim(block, 0, width, axis=dim), axis, backward)  7.07 us
    all_gather x1, blocking collectives, per_device(): bodies = lax.all_gather(top_coeff, 'top', axis=1, tiled=True)  5.17 us
    ppermute x3, starting transfers between devices, from_partner(): return lax.ppermute(block, axis, route)  3.57 us
    dot_general x3, matrix products, per_device(): jnp.einsum('rnk,nkj->rnj', coeffs[-1], transfer[first:first + members], p...  3.42 us
    gather x3, local copies, waits for them, and re-layouts, per_device(): picked = window[:, lists[first:first + members]]  1.72 us
    dot_general x3, matrix products, per_device(): jnp.einsum('rnsk,nskj->rnj', picked, coupling[first:first + members], pre...  1.56 us
  transfers between devices with their start and end apart: 12, of which 4 were waited for; matrix products, arithmetic and copies ran while one was open for 7% of the time, Pallas kernels for 0%

commit v1 on v0

v1 whole, which is shorter than its diff:
```python
import jax
import jax.numpy as jnp
from jax import lax
from jax.experimental import pallas as pl
from jax.experimental.pallas import tpu as pltpu
from jax.sharding import PartitionSpec as P

NEAR = 4
HIGH = lax.Precision.HIGH
VMEM = pltpu.MemorySpace.VMEM
SMEM = pltpu.MemorySpace.SMEM


def mm(a, b):
    return lax.dot_general(
        a, b, (((1,), (0,)), ((), ())), precision=HIGH, preferred_element_type=jnp.float32
    )


def mm_t(a, b):
    return lax.dot_general(
        a, b, (((1,), (1,)), ((), ())), precision=HIGH, preferred_element_type=jnp.float32
    )


def beside(a, b):
    return jnp.concatenate([a, b], axis=1)


def fold(x):
    half = x.shape[0] // 2
    return beside(x[:half], x[half:])


def unfold(x):
    half = x.shape[1] // 2
    return jnp.concatenate([x[:, :half], x[:, half:]], axis=0)


def tier_span(leaves, height):
    members = leaves >> height
    return 2 * leaves - 2 * members, members


def path_product(coarse_ref, position, tiers):
    product = None
    products = []
    for tier in range(tiers):
        matrix = coarse_ref[0, tier, (position >> tier) & 1]
        product = matrix if product is None else mm(product, matrix)
        products.append(product)
    return products


def up_kernel(charges, basis, transfer, coarse_transfer, ahead, behind, exchange):
    leaves, points = basis.shape[1], basis.shape[2]
    levels = leaves.bit_length() - 1
    position = lax.axis_index("leaf")
    body = lax.axis_index("top")
    top_count = exchange.shape[1]
    width = 2 * points
    reach = NEAR * points // width
    whole = leaves // 2
    pairs = leaves - 1
    for k in range(reach):
        first = (whole - reach + k) * width
        ahead[pairs + k] = charges[0, :, first : first + width]
        behind[pairs + k] = charges[0, :, k * width : (k + 1) * width]
    product = path_product(coarse_transfer, position, coarse_transfer.shape[1])[-1]
    coeffs = [mm(charges[0, :, g * points : (g + 1) * points], basis[0, g]) for g in range(leaves)]
    for height in range(levels):
        first, members = tier_span(leaves, height)
        for j in range(members // 2):
            pair = beside(coeffs[2 * j], coeffs[2 * j + 1])
            ahead[first // 2 + j] = pair
            behind[first // 2 + j] = pair
        coeffs = [
            mm(coeffs[2 * j], transfer[0, first + 2 * j])
            + mm(coeffs[2 * j + 1], transfer[0, first + 2 * j + 1])
            for j in range(members // 2)
        ]
    own = fold(coeffs[0])
    other = fold(mm(coeffs[0], product))
    for t in range(top_count):
        value = jnp.where(body == t, own, other)
        exchange[:, t] = jnp.broadcast_to(value[None], (exchange.shape[0],) + value.shape)


def middle_kernel(
    near_list,
    coupling_list,
    charges,
    basis,
    near_blocks,
    transfer,
    coupling,
    coarse_transfer,
    coarse_coupling,
    opposite,
    body_coupling,
    mine,
    below,
    above,
    known,
    mats,
    path,
    window,
    sources,
):
    leaves, points = basis.shape[1], basis.shape[2]
    rank = basis.shape[3]
    rhs = charges.shape[1]
    levels = leaves.bit_length() - 1
    position = lax.axis_index("leaf")
    coarse = coarse_transfer.shape[1]
    pairs = leaves - 1
    width = 2 * points
    reach = NEAR * points // width
    low_lanes = lax.broadcasted_iota(jnp.int32, (rhs, width), 1) < points

    def spread(pair, ref, even, odd):
        turned = pltpu.roll(pair, points, 1)
        ref[even] = jnp.where(low_lanes, pair, turned)
        ref[odd] = jnp.where(low_lanes, turned, pair)

    for k in range(reach):
        spread(below[pairs + k], sources, 2 * k, 2 * k + 1)
        at = NEAR + leaves + 2 * k
        spread(above[pairs + k], sources, at, at + 1)
    for k in range(leaves // 2):
        at = NEAR + 2 * k
        spread(charges[0, :, k * width : (k + 1) * width], sources, at, at + 1)
    for height in range(levels):
        first, members = tier_span(leaves, height)
        for block, pack in enumerate((below, mine, above)):
            for j in range(members // 2):
                at = 3 * first + block * members + 2 * j
                spread(pack[first // 2 + j], window, at, at + 1)

    def three(ref, base, list_ref, n):
        a = ref[base + list_ref[0, n, 0]]
        b = ref[base + list_ref[0, n, 1]]
        c = ref[base + list_ref[0, n, 2]]
        return beside(jnp.where(low_lanes, a, b), c[:, :points])

    near = []
    for g in range(leaves):
        left = three(sources, g, near_list, g)
        near.append(mm(left, near_blocks[0, g].reshape(3 * points, points)))
    local = None
    for height in range(levels - 1, -1, -1):
        first, members = tier_span(leaves, height)
        now = []
        for n in range(members):
            left = three(window, 3 * first, coupling_list, first + n)
            value = mm(left, coupling[0, first + n].reshape(3 * rank, rank))
            if local is not None:
                value = value + mm_t(local[n // 2], transfer[0, first + n])
            now.append(value)
        local = now
    for j in range(leaves // 2):
        value = [near[g] + mm_t(local[g], basis[0, g]) for g in (2 * j, 2 * j + 1)]
        known[:, j * width : (j + 1) * width] = beside(value[0], value[1])

    composite = None
    for height in range(levels - 1, -1, -1):
        first, members = tier_span(leaves, height)
        if composite is None:
            composite = [transfer[0, first + n] for n in range(members)]
        else:
            composite = [mm(transfer[0, first + n], composite[n // 2]) for n in range(members)]
    for g in range(leaves):
        path[g * points : (g + 1) * points] = mm(basis[0, g], composite[g])

    products = path_product(coarse_transfer, position, coarse)
    at = 0

    def put(value):
        nonlocal at
        mats[at : at + rank] = value
        at += rank

    for s in range(body_coupling.shape[1]):
        put(mm_t(body_coupling[0, s], products[coarse - 1]))
    for tier in range(coarse - 2):
        odd = (position >> tier) & 1
        for slot in (1, 2, jnp.where(odd == 1, 0, 3)):
            value = coarse_coupling[0, tier, slot]
            put(value if tier == 0 else mm_t(value, products[tier - 1]))
    far = mm_t(opposite[0], products[coarse - 3])
    put(mm(coarse_transfer[0, coarse - 3, 0], far))
    put(mm(coarse_transfer[0, coarse - 3, 1], far))


def final_kernel(received, known, mats, path, coarse_transfer, out, *tier_refs):
    leaf_count, top_count = received.shape[0], received.shape[1]
    coarse = coarse_transfer.shape[1]
    rhs = out.shape[1]
    position = lax.axis_index("leaf")
    body = lax.axis_index("top")
    terms = []
    for s in range(top_count - 1):
        other = lax.rem(body + 1 + s, top_count)
        total = received[0, other]
        for j in range(1, leaf_count):
            total = total + received[j, other]
        terms.append(unfold(total))

    def node(tier, index):
        if tier == 0:
            return unfold(received[index, body])
        return tier_refs[tier - 1][index]

    for tier in range(coarse - 2):
        count = leaf_count >> tier
        here = position >> tier
        odd = here & 1
        for offset in (-2, 2, jnp.where(odd == 1, -3, 3)):
            terms.append(node(tier, (here + offset + count) & (count - 1)))
        if tier < coarse - 3:
            for j in range(count // 2):
                tier_refs[tier][j] = mm(node(tier, 2 * j), coarse_transfer[0, tier, 0]) + mm(
                    node(tier, 2 * j + 1), coarse_transfer[0, tier, 1]
                )
    across = ((position >> (coarse - 2)) + 2) & 3
    terms.append(node(coarse - 3, 2 * across))
    terms.append(node(coarse - 3, 2 * across + 1))
    local = mm(jnp.concatenate(terms, axis=1), mats[...])
    out[0] = known[...] + mm_t(local, path[...])


def per_device(
    charges,
    leaf_basis,
    near_blocks,
    near_list,
    local_transfer,
    local_coupling,
    coupling_list,
    coarse_transfer,
    coarse_coupling,
    opposite_coupling,
    body_coupling,
):
    rhs = charges.shape[1]
    leaves, points, rank = leaf_basis.shape[1:]
    leaf_count = lax.axis_size("leaf")
    top_count = lax.axis_size("top")
    coarse = coarse_transfer.shape[1]
    packs = leaves - 1 + NEAR // 2
    f32 = jnp.float32
    vmem = pl.BlockSpec(memory_space=VMEM)
    smem = pl.BlockSpec(memory_space=SMEM)
    pack_shape = jax.ShapeDtypeStruct((packs, rhs, 2 * rank), f32)
    ahead, behind, exchange = pl.pallas_call(
        up_kernel,
        out_shape=(
            pack_shape,
            pack_shape,
            jax.ShapeDtypeStruct((leaf_count, top_count, rhs // 2, 2 * rank), f32),
        ),
        in_specs=[vmem] * 4,
        out_specs=(vmem,) * 3,
        name="up",
        cost_estimate=pl.CostEstimate(flops=40_000_000, bytes_accessed=1_000_000, transcendentals=0),
    )(charges, leaf_basis, local_transfer, coarse_transfer)
    forward = [(i, (i + 1) % leaf_count) for i in range(leaf_count)]
    backward = [(target, source) for source, target in forward]
    below = lax.ppermute(ahead, "leaf", forward)
    above = lax.ppermute(behind, "leaf", backward)
    received = lax.all_to_all(
        exchange.reshape(leaf_count * top_count, rhs // 2, 2 * rank),
        ("leaf", "top"),
        0,
        0,
        tiled=True,
    ).reshape(exchange.shape)
    terms = (top_count - 1) + 3 * (coarse - 2) + 2
    known, mats, path = pl.pallas_call(
        middle_kernel,
        out_shape=(
            jax.ShapeDtypeStruct((rhs, leaves * points), f32),
            jax.ShapeDtypeStruct((terms * rank, rank), f32),
            jax.ShapeDtypeStruct((leaves * points, rank), f32),
        ),
        in_specs=[smem] * 2 + [vmem] * 12,
        out_specs=(vmem,) * 3,
        scratch_shapes=[
            pltpu.VMEM((3 * (2 * leaves - 2), rhs, 2 * rank), f32),
            pltpu.VMEM((leaves + 2 * NEAR, rhs, 2 * points), f32),
        ],
        name="middle",
        cost_estimate=pl.CostEstimate(flops=80_000_000, bytes_accessed=3_000_000, transcendentals=0),
    )(
        near_list,
        coupling_list,
        charges,
        leaf_basis,
        near_blocks,
        local_transfer,
        local_coupling,
        coarse_transfer,
        coarse_coupling,
        opposite_coupling,
        body_coupling,
        ahead,
        below,
        above,
    )
    return pl.pallas_call(
        final_kernel,
        out_shape=jax.ShapeDtypeStruct(charges.shape, f32),
        in_specs=[vmem] * 5,
        out_specs=vmem,
        scratch_shapes=[
            pltpu.VMEM((leaf_count >> (tier + 1), rhs, rank), f32) for tier in range(coarse - 3)
        ],
        name="final",
        cost_estimate=pl.CostEstimate(flops=10_000_000, bytes_accessed=600_000, transcendentals=0),
    )(received, known, mats, path, coarse_transfer)


def solution(mesh):
    in_specs = (
        P("top", None, "leaf"),
        P("top", "leaf", None, None),
        P("top", "leaf", None, None, None),
        P("top", "leaf", None),
        P("top", "leaf", None, None),
        P("top", "leaf", None, None, None),
        P("top", "leaf", None),
        P("top", None, None, None, None),
        P("top", None, None, None, None),
        P("top", None, None),
        P("top", None, None, None),
    )
    out_specs = P("top", None, "leaf")
    return jax.shard_map(
        per_device, mesh=mesh, in_specs=in_specs, out_specs=out_specs, check_vma=False
    )
```

time: 51.5 us -> 31.3 us (0.61)
  matrix products: 10.6 us -> 0 us
  Pallas kernels: 0 us -> 10.5 us
  starting transfers between devices: 21.7 us -> 11.9 us
  blocking collectives: 5.17 us -> 0 us
  waiting for transfers between devices: 8.2 us -> 4.56 us
  local copies, waits for them, and re-layouts: 4.95 us -> 3.97 us
    ppermute x12 -> x2, starting transfers between devices: 21.7 us -> 4.61 us  [the longest x1 4.6 us: per_device(): above = lax.ppermute(behind, 'leaf', backward)]
    dot_general x26 -> x0, matrix products: 10.6 us -> none  [the longest x3 3.42 us: per_device(): jnp.einsum('rnk,nkj->rnj', coeffs[-1], transfer[first:first + members], p...]
    pallas_call x0 -> x3, Pallas kernels: none -> 10.5 us  [the longest x1 5.39 us: per_device(): pl.pallas_call(middle_kernel, out_shape=(jax.ShapeDtypeStruct((rhs, leave...]
    all_to_all x0 -> x1, starting transfers between devices: none -> 7.33 us  [per_device(): lax.all_to_all(exchange.reshape(leaf_count * top_count, rhs // 2, 2 * ran...]
    all_gather x1 -> x0, blocking collectives: 5.17 us -> none  [per_device(): bodies = lax.all_gather(top_coeff, 'top', axis=1, tiled=True)]
    unnamed x24 -> x8, local copies, waits for them, and re-layouts: 0.06 us -> 3.97 us
    ppermute x12 -> x2, waiting for transfers between devices: 8.2 us -> 4.55 us  [the longest x1 4.55 us: per_device(): below = lax.ppermute(ahead, 'leaf', forward)]
    gather x4 -> x0, local copies, waits for them, and re-layouts: 2.3 us -> none  [the longest x3 1.72 us: per_device(): picked = window[:, lists[first:first + members]]]
  transfers between devices with their start and end apart: 12 -> 3, of which waited for: 4 -> 1; matrix products, arithmetic and copies ran while one was open for 7% -> 9% of each run, Pallas kernels for 0% -> 17%
where the time goes in v1:
time: 31.3 us; the launch traced here: 31 us
  starting transfers between devices  11.9 us (38%)
  Pallas kernels  10.5 us (34%)
  waiting for transfers between devices  4.56 us (15%)
  local copies, waits for them, and re-layouts  3.97 us (13%)
    all_to_all x1, starting transfers between devices, per_device(): lax.all_to_all(exchange.reshape(leaf_count * top_count, rhs // 2, 2 * ran...  7.33 us
    pallas_call x1, Pallas kernels, per_device(): pl.pallas_call(middle_kernel, out_shape=(jax.ShapeDtypeStruct((rhs, leave...  5.39 us
    ppermute x1, starting transfers between devices, per_device(): above = lax.ppermute(behind, 'leaf', backward)  4.6 us
    ppermute x1, waiting for transfers between devices, per_device(): below = lax.ppermute(ahead, 'leaf', forward)  4.55 us
    unnamed x8, local copies, waits for them, and re-layouts  3.97 us
    pallas_call x1, Pallas kernels, per_device(): pl.pallas_call(up_kernel, out_shape=(pack_shape, pack_shape, jax.ShapeDty...  2.88 us
    pallas_call x1, Pallas kernels, per_device(): pl.pallas_call(final_kernel, out_shape=jax.ShapeDtypeStruct(charges.shape...  2.26 us
  transfers between devices with their start and end apart: 3, of which 1 were waited for; matrix products, arithmetic and copies ran while one was open for 9% of the time, Pallas kernels for 17%

profile of v1, /device:TPU:0, one launch (start us, length us, event | category | flops | bytes accessed | tf_op | source)
XLA Modules:
  0.0 31.0 jit_solution(9996454575710747903)
XLA Ops:
  0.0 2.9 %up.1 = (f32[9,16,128]{2,1,0:T(8,128)}, f32[9,16,128]{2,1,0:T(8,128)}, f32[8,4,8,128]{3,2,1,0:T(8,128)}) custom-call(f32[1,16,512]{2,1,0:T(8,128)} %charges.3, f32[1,8,64,64]{3,2,1,0:T(8,128)} %basis.3, f32[1,14,64,64]{3,2,1,0:T(8,128)} %transfer.3, f32[1,3,2,64,64]{4,3,2,1,0:T(8,128)} %coarse_transfer.5), custom_call_target="tpu_custom_call" | custom-call | flops 40000000 | bytes 1000000 | tf_op jit(solution)/shard_map/up/pallas_call | solution.py:255
  2.9 7.3 %all-to-all-start = ((f32[32,8,128]{2,1,0:T(8,128)}), f32[32,8,128]{2,1,0:T(8,128)S(1)}, u32[]{:S(2)}, u32[]{:S(2)}) async-start(f32[32,8,128]{2,1,0:T(8,128)} %bitcast.3), calls=%async_computation | async-start | bytes 262144 | tf_op jit(solution)/shard_map/all_to_all | solution.py:271
  10.2 4.6 %collective-permute-start.1 = (f32[9,16,128]{2,1,0:T(8,128)}, f32[9,16,128]{2,1,0:T(8,128)S(1)}, u32[]{:S(2)}, u32[]{:S(2)}) collective-permute-start(f32[9,16,128]{2,1,0:T(8,128)} %get-tuple-element.13), channel_id=1, source_target_pairs={{4,0},{8,4},{12,8},{16,12},{20,16},{24,20},{28,24},{0,28},{5,1},{9... | collective-permute-start | bytes 221192 | tf_op jit(solution)/shard_map/ppermute | solution.py:270
  14.8 0.0 collective-permute-start
  14.8 1.3 %copy.12.near_list = s32[1,8,3]{2,1,0:T(8,128)} copy(s32[1,8,3]{1,0,2:T(1,128)} %param.14) | data formatting | bytes 192 | tf_op args[3]
  16.2 1.4 %copy.13.coupling_list = s32[1,14,3]{2,1,0:T(8,128)} copy(s32[1,14,3]{1,0,2:T(1,128)} %param.17) | data formatting | bytes 336 | tf_op args[6]
  17.5 0.0 collective-permute-done.1.above
  17.5 0.0 copy-start.1
  17.5 4.6 %collective-permute-done.below = f32[9,16,128]{2,1,0:T(8,128)S(1)} collective-permute-done((f32[9,16,128]{2,1,0:T(8,128)}, f32[9,16,128]{2,1,0:T(8,128)S(1)}, u32[]{:S(2)}, u32[]{:S(2)}) %collective-permute-start) | collective-permute-done | bytes 73760 | tf_op jit(solution)/shard_map/ppermute | solution.py:269
  22.1 0.0 copy-done.1
  22.1 0.0 copy-start.2
  22.1 0.6 %copy-done.2 = f32[9,16,128]{2,1,0:T(8,128)} copy-done((f32[9,16,128]{2,1,0:T(8,128)}, f32[9,16,128]{2,1,0:T(8,128)S(1)}, u32[]{:S(2)}) %copy-start.2) | copy-done | bytes 73752
  22.7 5.4 %middle.1 = (f32[16,512]{1,0:T(8,128)}, f32[512,64]{1,0:T(8,128)}, f32[512,64]{1,0:T(8,128)}) custom-call(s32[1,8,3]{2,1,0:T(8,128)} %copy.12.near_list, s32[1,14,3]{2,1,0:T(8,128)} %copy.13.coupling_list, f32[1,16,512]{2,1,0:T(8,128)} %charges.3, f32[1,8,64,64]{3,2,1,0:T(8,128)} %basis.3, f32[1,8,3,64,64]{4,3,2,1,0:T(8,128)} %near_blocks.1, ...), custom_call_target="tpu_custom_call" | custom-call | flops 80000000 | bytes 3000000 | tf_op jit(solution)/shard_map/middle/pallas_call | solution.py:279
  28.1 0.0 all-to-all-done
  28.1 0.0 copy-start
  28.1 0.6 %copy-done = f32[32,8,128]{2,1,0:T(8,128)} copy-done((f32[32,8,128]{2,1,0:T(8,128)}, f32[32,8,128]{2,1,0:T(8,128)S(1)}, u32[]{:S(2)}) %copy-start) | copy-done | bytes 131096
  28.8 2.3 %final.1 = f32[1,16,512]{2,1,0:T(8,128)} custom-call(f32[8,4,8,128]{3,2,1,0:T(8,128)} %bitcast.2, f32[16,512]{1,0:T(8,128)} %get-tuple-element.14.known, f32[512,64]{1,0:T(8,128)} %get-tuple-element.15.mats, f32[512,64]{1,0:T(8,128)} %get-tuple-element.16.path, f32[1,3,2,64,64]{4,3,2,1,0:T(8,128)} %coarse_transfer.5), custom_call_target="tpu_custom_call" | custom-call | flops 10000000 | bytes 600000 | tf_op jit(solution)/shard_map/final/pallas_call | solution.py:310
Async XLA Ops:
  2.9 25.2 %all-to-all-start = ((f32[32,8,128]{2,1,0:T(8,128)}), f32[32,8,128]{2,1,0:T(8,128)S(1)}, u32[]{:S(2)}, u32[]{:S(2)}) async-start(f32[32,8,128]{2,1,0:T(8,128)} %bitcast.3), calls=%async_computation | async-start | bytes 262144 | tf_op jit(solution)/shard_map/all_to_all | solution.py:271
  10.2 7.3 %collective-permute-start.1 = (f32[9,16,128]{2,1,0:T(8,128)}, f32[9,16,128]{2,1,0:T(8,128)S(1)}, u32[]{:S(2)}, u32[]{:S(2)}) collective-permute-start(f32[9,16,128]{2,1,0:T(8,128)} %get-tuple-element.13), channel_id=1, source_target_pairs={{4,0},{8,4},{12,8},{16,12},{20,16},{24,20},{28,24},{0,28},{5,1},{9... | collective-permute-start | bytes 221192 | tf_op jit(solution)/shard_map/ppermute | solution.py:270
  14.8 7.3 %collective-permute-start = (f32[9,16,128]{2,1,0:T(8,128)}, f32[9,16,128]{2,1,0:T(8,128)S(1)}, u32[]{:S(2)}, u32[]{:S(2)}) collective-permute-start(f32[9,16,128]{2,1,0:T(8,128)} %get-tuple-element.12.mine), channel_id=1, source_target_pairs={{0,4},{4,8},{8,12},{12,16},{16,20},{20,24},{24,28},{28,0},{1,5},{5... | collective-permute-start | bytes 221192 | tf_op jit(solution)/shard_map/ppermute | solution.py:269
  17.5 4.6 %copy-start.1 = (f32[9,16,128]{2,1,0:T(8,128)}, f32[9,16,128]{2,1,0:T(8,128)S(1)}, u32[]{:S(2)}) copy-start(f32[9,16,128]{2,1,0:T(8,128)S(1)} %collective-permute-done.1.above) | copy-start | bytes 221188
  22.1 0.6 %copy-start.2 = (f32[9,16,128]{2,1,0:T(8,128)}, f32[9,16,128]{2,1,0:T(8,128)S(1)}, u32[]{:S(2)}) copy-start(f32[9,16,128]{2,1,0:T(8,128)S(1)} %collective-permute-done.below) | copy-start | bytes 221188
  28.1 0.7 %copy-start = (f32[32,8,128]{2,1,0:T(8,128)}, f32[32,8,128]{2,1,0:T(8,128)S(1)}, u32[]{:S(2)}) copy-start(f32[32,8,128]{2,1,0:T(8,128)S(1)} %all-to-all-done) | copy-start | bytes 393220

commit v2 on v1

--- a/solution.py
+++ b/solution.py
@@ -9,6 +9,7 @@
 HIGH = lax.Precision.HIGH
 VMEM = pltpu.MemorySpace.VMEM
 SMEM = pltpu.MemorySpace.SMEM
+HBM = pltpu.MemorySpace.HBM
 
 
 def mm(a, b):
@@ -52,7 +53,35 @@
     return products
 
 
-def up_kernel(charges, basis, transfer, coarse_transfer, ahead, behind, exchange):
+def fetch(sources, targets, sem):
+    copies = [
+        pltpu.make_async_copy(source, target, sem.at[i])
+        for i, (source, target) in enumerate(zip(sources, targets))
+    ]
+    for copy in copies:
+        copy.start()
+    return copies
+
+
+def up_kernel(
+    charges_hbm,
+    basis_hbm,
+    transfer_hbm,
+    coarse_hbm,
+    ahead,
+    behind,
+    exchange,
+    charges,
+    basis,
+    transfer,
+    coarse_transfer,
+    sem,
+):
+    copies = fetch(
+        (charges_hbm, basis_hbm, coarse_hbm, transfer_hbm),
+        (charges, basis, coarse_transfer, transfer),
+        sem,
+    )
     leaves, points = basis.shape[1], basis.shape[2]
     levels = leaves.bit_length() - 1
     position = lax.axis_index("leaf")
@@ -62,11 +91,15 @@
     reach = NEAR * points // width
     whole = leaves // 2
     pairs = leaves - 1
+    copies[0].wait()
+    copies[1].wait()
     for k in range(reach):
         first = (whole - reach + k) * width
         ahead[pairs + k] = charges[0, :, first : first + width]
         behind[pairs + k] = charges[0, :, k * width : (k + 1) * width]
+    copies[2].wait()
     product = path_product(coarse_transfer, position, coarse_transfer.shape[1])[-1]
+    copies[3].wait()
     coeffs = [mm(charges[0, :, g * points : (g + 1) * points], basis[0, g]) for g in range(leaves)]
     for height in range(levels):
         first, members = tier_span(leaves, height)
@@ -86,33 +119,84 @@
         exchange[:, t] = jnp.broadcast_to(value[None], (exchange.shape[0],) + value.shape)
 
 
-def middle_kernel(
+def prep_kernel(
+    basis,
+    transfer,
+    coarse_transfer,
+    coarse_coupling_hbm,
+    opposite_hbm,
+    body_coupling_hbm,
+    near_hbm,
+    coupling_hbm,
+    mats,
+    local_path,
+    path,
+    near_blocks,
+    coupling,
+    coarse_coupling,
+    opposite,
+    body_coupling,
+    sem,
+):
+    copies = fetch(
+        (coarse_coupling_hbm, opposite_hbm, body_coupling_hbm, near_hbm, coupling_hbm),
+        (coarse_coupling, opposite, body_coupling, near_blocks, coupling),
+        sem,
+    )
+    leaves, points, rank = basis.shape[1:]
+    levels = leaves.bit_length() - 1
+    position = lax.axis_index("leaf")
+    coarse = coarse_transfer.shape[1]
+    for g in range(leaves):
+        product = basis[0, g]
+        for height in range(levels):
+            local_path[g, height * rank : (height + 1) * rank] = product.T
+            first, _ = tier_span(leaves, height)
+            product = mm(product, transfer[0, first + (g >> height)])
+        path[g] = product.T
+
+    products = path_product(coarse_transfer, position, coarse)
+    at = 0
+
+    def put(value):
+        nonlocal at
+        mats[at : at + rank] = value
+        at += rank
+
+    for copy in copies[:3]:
+        copy.wait()
+    for s in range(body_coupling.shape[1]):
+        put(mm_t(body_coupling[0, s], products[coarse - 1]))
+    for tier in range(coarse - 2):
+        odd = (position >> tier) & 1
+        for slot in (1, 2, jnp.where(odd == 1, 0, 3)):
+            value = coarse_coupling[0, tier, slot]
+            put(value if tier == 0 else mm_t(value, products[tier - 1]))
+    far = mm_t(opposite[0], products[coarse - 3])
+    put(mm(coarse_transfer[0, coarse - 3, 0], far))
+    put(mm(coarse_transfer[0, coarse - 3, 1], far))
+    for copy in copies[3:]:
+        copy.wait()
+
+
+def near_kernel(
     near_list,
     coupling_list,
     charges,
-    basis,
     near_blocks,
-    transfer,
     coupling,
-    coarse_transfer,
-    coarse_coupling,
-    opposite,
-    body_coupling,
+    local_path,
     mine,
     below,
     above,
     known,
-    mats,
-    path,
     window,
     sources,
 ):
-    leaves, points = basis.shape[1], basis.shape[2]
-    rank = basis.shape[3]
+    leaves, points = near_blocks.shape[1], near_blocks.shape[3]
+    rank = coupling.shape[3]
     rhs = charges.shape[1]
     levels = leaves.bit_length() - 1
-    position = lax.axis_index("leaf")
-    coarse = coarse_transfer.shape[1]
     pairs = leaves - 1
     width = 2 * points
     reach = NEAR * points // width
@@ -138,58 +222,24 @@
                 spread(pack[first // 2 + j], window, at, at + 1)
 
     def three(ref, base, list_ref, n):
-        a = ref[base + list_ref[0, n, 0]]
-        b = ref[base + list_ref[0, n, 1]]
-        c = ref[base + list_ref[0, n, 2]]
+        a = ref[base + list_ref[0, 0, n]]
+        b = ref[base + list_ref[1, 0, n]]
+        c = ref[base + list_ref[2, 0, n]]
         return beside(jnp.where(low_lanes, a, b), c[:, :points])
 
-    near = []
+    coupled = []
+    for n in range(2 * leaves - 2):
+        height = next(h for h in range(levels) if n < sum(tier_span(leaves, h)))
+        left = three(window, 3 * tier_span(leaves, height)[0], coupling_list, n)
+        coupled.append(mm(left, coupling[0, n].reshape(3 * rank, rank)))
+    result = []
     for g in range(leaves):
         left = three(sources, g, near_list, g)
-        near.append(mm(left, near_blocks[0, g].reshape(3 * points, points)))
-    local = None
-    for height in range(levels - 1, -1, -1):
-        first, members = tier_span(leaves, height)
-        now = []
-        for n in range(members):
-            left = three(window, 3 * first, coupling_list, first + n)
-            value = mm(left, coupling[0, first + n].reshape(3 * rank, rank))
-            if local is not None:
-                value = value + mm_t(local[n // 2], transfer[0, first + n])
-            now.append(value)
-        local = now
+        value = mm(left, near_blocks[0, g].reshape(3 * points, points))
+        chain = [coupled[tier_span(leaves, h)[0] + (g >> h)] for h in range(levels)]
+        result.append(value + mm(jnp.concatenate(chain, axis=1), local_path[g]))
     for j in range(leaves // 2):
-        value = [near[g] + mm_t(local[g], basis[0, g]) for g in (2 * j, 2 * j + 1)]
-        known[:, j * width : (j + 1) * width] = beside(value[0], value[1])
-
-    composite = None
-    for height in range(levels - 1, -1, -1):
-        first, members = tier_span(leaves, height)
-        if composite is None:
-            composite = [transfer[0, first + n] for n in range(members)]
-        else:
-            composite = [mm(transfer[0, first + n], composite[n // 2]) for n in range(members)]
-    for g in range(leaves):
-        path[g * points : (g + 1) * points] = mm(basis[0, g], composite[g])
-
-    products = path_product(coarse_transfer, position, coarse)
-    at = 0
-
-    def put(value):
-        nonlocal at
-        mats[at : at + rank] = value
-        at += rank
-
-    for s in range(body_coupling.shape[1]):
-        put(mm_t(body_coupling[0, s], products[coarse - 1]))
-    for tier in range(coarse - 2):
-        odd = (position >> tier) & 1
-        for slot in (1, 2, jnp.where(odd == 1, 0, 3)):
-            value = coarse_coupling[0, tier, slot]
-            put(value if tier == 0 else mm_t(value, products[tier - 1]))
-    far = mm_t(opposite[0], products[coarse - 3])
-    put(mm(coarse_transfer[0, coarse - 3, 0], far))
-    put(mm(coarse_transfer[0, coarse - 3, 1], far))
+        known[:, j * width : (j + 1) * width] = beside(result[2 * j], result[2 * j + 1])
 
 
 def final_kernel(received, known, mats, path, coarse_transfer, out, *tier_refs):
@@ -226,7 +276,11 @@
     terms.append(node(coarse - 3, 2 * across))
     terms.append(node(coarse - 3, 2 * across + 1))
     local = mm(jnp.concatenate(terms, axis=1), mats[...])
-    out[0] = known[...] + mm_t(local, path[...])
+    points = path.shape[2]
+    for j in range(path.shape[0] // 2):
+        at = 2 * j * points
+        value = beside(mm(local, path[2 * j]), mm(local, path[2 * j + 1]))
+        out[0, :, at : at + 2 * points] = known[:, at : at + 2 * points] + value
 
 
 def per_device(
@@ -251,19 +305,31 @@
     f32 = jnp.float32
     vmem = pl.BlockSpec(memory_space=VMEM)
     smem = pl.BlockSpec(memory_space=SMEM)
+    params = pltpu.CompilerParams(vmem_limit_bytes=8 << 20)
     pack_shape = jax.ShapeDtypeStruct((packs, rhs, 2 * rank), f32)
-    ahead, behind, exchange = pl.pallas_call(
+    hbm = pl.BlockSpec(memory_space=HBM)
+
+    def like(*arrays):
+        return tuple(jax.ShapeDtypeStruct(array.shape, array.dtype) for array in arrays)
+
+    def stay(*arrays):
+        return [pltpu.with_memory_space_constraint(array, HBM) for array in arrays]
+
+    ahead, behind, exchange, charges_v, basis_v, transfer_v, coarse_v = pl.pallas_call(
         up_kernel,
         out_shape=(
             pack_shape,
             pack_shape,
             jax.ShapeDtypeStruct((leaf_count, top_count, rhs // 2, 2 * rank), f32),
-        ),
-        in_specs=[vmem] * 4,
-        out_specs=(vmem,) * 3,
+        )
+        + like(charges, leaf_basis, local_transfer, coarse_transfer),
+        in_specs=[hbm] * 4,
+        out_specs=(vmem,) * 7,
+        scratch_shapes=[pltpu.SemaphoreType.DMA((4,))],
         name="up",
+        compiler_params=params,
         cost_estimate=pl.CostEstimate(flops=40_000_000, bytes_accessed=1_000_000, transcendentals=0),
-    )(charges, leaf_basis, local_transfer, coarse_transfer)
+    )(*stay(charges, leaf_basis, local_transfer, coarse_transfer))
     forward = [(i, (i + 1) % leaf_count) for i in range(leaf_count)]
     backward = [(target, source) for source, target in forward]
     below = lax.ppermute(ahead, "leaf", forward)
@@ -276,33 +342,50 @@
         tiled=True,
     ).reshape(exchange.shape)
     terms = (top_count - 1) + 3 * (coarse - 2) + 2
-    known, mats, path = pl.pallas_call(
-        middle_kernel,
+    levels = leaves.bit_length() - 1
+    mats, local_path, path, near_v, coupling_v = pl.pallas_call(
+        prep_kernel,
         out_shape=(
-            jax.ShapeDtypeStruct((rhs, leaves * points), f32),
             jax.ShapeDtypeStruct((terms * rank, rank), f32),
-            jax.ShapeDtypeStruct((leaves * points, rank), f32),
-        ),
-        in_specs=[smem] * 2 + [vmem] * 12,
-        out_specs=(vmem,) * 3,
+            jax.ShapeDtypeStruct((leaves, levels * rank, points), f32),
+            jax.ShapeDtypeStruct((leaves, rank, points), f32),
+        )
+        + like(near_blocks, local_coupling),
+        in_specs=[vmem] * 3 + [hbm] * 5,
+        out_specs=(vmem,) * 5,
+        scratch_shapes=[
+            pltpu.VMEM(array.shape, f32)
+            for array in (coarse_coupling, opposite_coupling, body_coupling)
+        ]
+        + [pltpu.SemaphoreType.DMA((5,))],
+        name="prep",
+        compiler_params=params,
+        cost_estimate=pl.CostEstimate(flops=40_000_000, bytes_accessed=2_000_000, transcendentals=0),
+    )(
+        basis_v,
+        transfer_v,
+        coarse_v,
+        *stay(coarse_coupling, opposite_coupling, body_coupling, near_blocks, local_coupling),
+    )
+    known = pl.pallas_call(
+        near_kernel,
+        out_shape=jax.ShapeDtypeStruct((rhs, leaves * points), f32),
+        in_specs=[smem] * 2 + [vmem] * 7,
+        out_specs=vmem,
         scratch_shapes=[
             pltpu.VMEM((3 * (2 * leaves - 2), rhs, 2 * rank), f32),
             pltpu.VMEM((leaves + 2 * NEAR, rhs, 2 * points), f32),
         ],
-        name="middle",
+        name="near",
+        compiler_params=params,
         cost_estimate=pl.CostEstimate(flops=80_000_000, bytes_accessed=3_000_000, transcendentals=0),
     )(
-        near_list,
-        coupling_list,
-        charges,
-        leaf_basis,
-        near_blocks,
-        local_transfer,
-        local_coupling,
-        coarse_transfer,
-        coarse_coupling,
-        opposite_coupling,
-        body_coupling,
+        jnp.transpose(near_list, (2, 0, 1)),
+        jnp.transpose(coupling_list, (2, 0, 1)),
+        charges_v,
+        near_v,
+        coupling_v,
+        local_path,
         ahead,
         below,
         above,
@@ -316,8 +399,9 @@
             pltpu.VMEM((leaf_count >> (tier + 1), rhs, rank), f32) for tier in range(coarse - 3)
         ],
         name="final",
+        compiler_params=params,
         cost_estimate=pl.CostEstimate(flops=10_000_000, bytes_accessed=600_000, transcendentals=0),
-    )(received, known, mats, path, coarse_transfer)
+    )(received, known, mats, path, coarse_v)
 
 
 def solution(mesh):

time: 31.3 us -> 23.2 us (0.74)
  local copies, waits for them, and re-layouts: 3.97 us -> 0.01 us
  waiting for transfers between devices: 4.56 us -> 1.67 us
  Pallas kernels: 10.5 us -> 9.16 us
    unnamed x8 -> x4, local copies, waits for them, and re-layouts: 3.97 us -> 0.01 us
    ppermute x1, waiting for transfers between devices: 4.55 us -> 1.66 us  [per_device(): below = lax.ppermute(ahead, 'leaf', forward)]
    ppermute x1, starting transfers between devices: 0.01 us -> 1.82 us  [per_device(): below = lax.ppermute(ahead, 'leaf', forward)]
    ppermute x1, starting transfers between devices: 4.6 us -> 2.95 us  [per_device(): above = lax.ppermute(behind, 'leaf', backward)]
    pallas_call x1, Pallas kernels: 2.26 us -> 1.25 us  [per_device(): pl.pallas_call(final_kernel, out_shape=jax.ShapeDtypeStruct(charges.shape...]
    pallas_call x1 -> x2, Pallas kernels: 5.39 us -> 4.96 us  [the longest x1 2.92 us: per_device(): pl.pallas_call(prep_kernel, out_shape=(jax.ShapeDtypeStruct((terms * rank...]
  transfers between devices with their start and end apart: 3 -> 3, of which waited for: 1 -> 1; matrix products, arithmetic and copies ran while one was open for 9% -> 0% of each run, Pallas kernels for 17% -> 22%
where the time goes in v2:
time: 23.2 us; the launch traced here: 23 us
  starting transfers between devices  12.1 us (52%)
  Pallas kernels  9.16 us (39%)
  waiting for transfers between devices  1.67 us (7%)
    all_to_all x1, starting transfers between devices, per_device(): lax.all_to_all(exchange.reshape(leaf_count * top_count, rhs // 2, 2 * ran...  7.34 us
    ppermute x1, starting transfers between devices, per_device(): above = lax.ppermute(behind, 'leaf', backward)  2.95 us
    pallas_call x1, Pallas kernels, per_device(): pl.pallas_call(up_kernel, out_shape=(pack_shape, pack_shape, jax.ShapeDty...  2.95 us
    pallas_call x1, Pallas kernels, per_device(): pl.pallas_call(prep_kernel, out_shape=(jax.ShapeDtypeStruct((terms * rank...  2.92 us
    pallas_call x1, Pallas kernels, per_device(): pl.pallas_call(near_kernel, out_shape=jax.ShapeDtypeStruct((rhs, leaves *...  2.04 us
    ppermute x1, starting transfers between devices, per_device(): below = lax.ppermute(ahead, 'leaf', forward)  1.82 us
    ppermute x1, waiting for transfers between devices, per_device(): below = lax.ppermute(ahead, 'leaf', forward)  1.66 us
    pallas_call x1, Pallas kernels, per_device(): pl.pallas_call(final_kernel, out_shape=jax.ShapeDtypeStruct(charges.shape...  1.25 us
  transfers between devices with their start and end apart: 3, of which 1 were waited for; matrix products, arithmetic and copies ran while one was open for 0% of the time, Pallas kernels for 22%

profile of v2, /device:TPU:0, one launch (start us, length us, event | category | flops | bytes accessed | tf_op | source)
XLA Modules:
  0.0 23.0 jit_solution(5482141394634329973)
XLA Ops:
  0.0 2.9 %up.1 = (f32[9,16,128]{2,1,0:T(8,128)S(1)}, f32[9,16,128]{2,1,0:T(8,128)S(1)}, f32[8,4,8,128]{3,2,1,0:T(8,128)}, f32[1,16,512]{2,1,0:T(8,128)S(1)}, f32[1,8,64,6...) custom-call(f32[1,16,512]{2,1,0:T(8,128)} %charges_hbm.1, ...), custom_call_target="tpu_custom_call" | custom-call | flops 40000000 | bytes 1000000 | tf_op jit(solution)/shard_map/up/pallas_call | solution.py:318
  3.0 7.3 %all-to-all-start = ((f32[32,8,128]{2,1,0:T(8,128)}), f32[32,8,128]{2,1,0:T(8,128)S(1)}, u32[]{:S(2)}, u32[]{:S(2)}) async-start(f32[32,8,128]{2,1,0:T(8,128)} %bitcast), calls=%async_computation | async-start | bytes 262144 | tf_op jit(solution)/shard_map/all_to_all | solution.py:337
  10.3 1.8 %collective-permute-start = (f32[9,16,128]{2,1,0:T(8,128)S(1)}, f32[9,16,128]{2,1,0:T(8,128)S(1)}, u32[]{:S(2)}, u32[]{:S(2)}) collective-permute-start(f32[9,16,128]{2,1,0:T(8,128)S(1)} %get-tuple-element.25.mine), channel_id=1, source_target_pairs={{0,4},{4,8},{8,12},{12,16},{16,20},{20,24},{24,28},{28,0},{1,5},{5... | collective-permute-start | bytes 221192 | tf_op jit(solution)/shard_map/ppermute | solution.py:335
  12.1 3.0 %collective-permute-start.1 = (f32[9,16,128]{2,1,0:T(8,128)S(1)}, f32[9,16,128]{2,1,0:T(8,128)S(1)}, u32[]{:S(2)}, u32[]{:S(2)}) collective-permute-start(f32[9,16,128]{2,1,0:T(8,128)S(1)} %get-tuple-element.26), channel_id=1, source_target_pairs={{4,0},{8,4},{12,8},{16,12},{20,16},{24,20},{28,24},{0,28},{5,1},{9... | collective-permute-start | bytes 221192 | tf_op jit(solution)/shard_map/ppermute | solution.py:336
  15.1 0.0 copy-start
  15.1 0.0 copy-start.1
  15.1 2.9 %prep.1 = (f32[512,64]{1,0:T(8,128)S(1)}, f32[8,192,64]{2,1,0:T(8,128)S(1)}, f32[8,64,64]{2,1,0:T(8,128)S(1)}, f32[1,8,3,64,64]{4,3,2,1,0:T(8,128)S(1)}, f32[1,14,3,64,64]{4,3,2,1,0:T(8,128)S(1)}) custom-call(f32[1,8,64,64]{3,2,1,0:T(8,128)S(1)} %get-tuple-element.19.basis, f32[1,14,64,64]{3,2,1,0:T(8,128)S(1)} %get-tuple-element.20.transfer, ...), custom_call_target="tpu_custom_call" | custom-call | flops 40000000 | bytes 2000000 | tf_op jit(solution)/shard_map/prep/pallas_call | solution.py:346
  18.0 1.7 %collective-permute-done.below = f32[9,16,128]{2,1,0:T(8,128)S(1)} collective-permute-done((f32[9,16,128]{2,1,0:T(8,128)S(1)}, f32[9,16,128]{2,1,0:T(8,128)S(1)}, u32[]{:S(2)}, u32[]{:S(2)}) %collective-permute-start) | collective-permute-done | bytes 73760 | tf_op jit(solution)/shard_map/ppermute | solution.py:335
  19.7 0.0 collective-permute-done.1.above
  19.7 0.0 copy-done
  19.7 0.0 copy-done.1
  19.7 2.0 %near.1.known = f32[16,512]{1,0:T(8,128)S(1)} custom-call(s32[3,1,8]{2,1,0:T(1,128)S(1)} %bitcast.5, s32[3,1,14]{2,1,0:T(1,128)S(1)} %bitcast.6, f32[1,16,512]{2,1,0:T(8,128)S(1)} %get-tuple-element.18.charges, f32[1,8,3,64,64]{4,3,2,1,0:T(8,128)S(1)} %get-tuple-element.22.near_blocks, f32[1,14,3,64,64]{4,3,2,1,0:T(8,128)S(1)} %get-tuple-element.23.coupling, ...), custom_call_target="tpu_custom_call" | custom-call | flops 80000000 | bytes 3000000 | tf_op jit(solution)/shard_map/near/pallas_call | solution.py:370
  21.7 0.0 all-to-all-done
  21.7 1.3 %final.1 = f32[1,16,512]{2,1,0:T(8,128)} custom-call(f32[8,4,8,128]{3,2,1,0:T(8,128)S(1)} %bitcast.4, f32[16,512]{1,0:T(8,128)S(1)} %near.1.known, f32[512,64]{1,0:T(8,128)S(1)} %get-tuple-element.27.mats, f32[8,64,64]{2,1,0:T(8,128)S(1)} %get-tuple-element.28.path, f32[1,3,2,64,64]{4,3,2,1,0:T(8,128)S(1)} %get-tuple-element.21.coarse_transfer), custom_call_target="tpu_custom_call" | custom-call | flops 10000000 | bytes 600000 | tf_op jit(solution)/shard_map/final/pallas_call | solution.py:393
Async XLA Ops:
  3.0 18.8 %all-to-all-start = ((f32[32,8,128]{2,1,0:T(8,128)}), f32[32,8,128]{2,1,0:T(8,128)S(1)}, u32[]{:S(2)}, u32[]{:S(2)}) async-start(f32[32,8,128]{2,1,0:T(8,128)} %bitcast), calls=%async_computation | async-start | bytes 262144 | tf_op jit(solution)/shard_map/all_to_all | solution.py:337
  10.3 9.4 %collective-permute-start = (f32[9,16,128]{2,1,0:T(8,128)S(1)}, f32[9,16,128]{2,1,0:T(8,128)S(1)}, u32[]{:S(2)}, u32[]{:S(2)}) collective-permute-start(f32[9,16,128]{2,1,0:T(8,128)S(1)} %get-tuple-element.25.mine), channel_id=1, source_target_pairs={{0,4},{4,8},{8,12},{12,16},{16,20},{20,24},{24,28},{28,0},{1,5},{5... | collective-permute-start | bytes 221192 | tf_op jit(solution)/shard_map/ppermute | solution.py:335
  12.1 7.6 %collective-permute-start.1 = (f32[9,16,128]{2,1,0:T(8,128)S(1)}, f32[9,16,128]{2,1,0:T(8,128)S(1)}, u32[]{:S(2)}, u32[]{:S(2)}) collective-permute-start(f32[9,16,128]{2,1,0:T(8,128)S(1)} %get-tuple-element.26), channel_id=1, source_target_pairs={{4,0},{8,4},{12,8},{16,12},{20,16},{24,20},{28,24},{0,28},{5,1},{9... | collective-permute-start | bytes 221192 | tf_op jit(solution)/shard_map/ppermute | solution.py:336
  15.1 4.6 %copy-start = (s32[1,8,3]{1,0,2:T(1,128)S(1)}, s32[1,8,3]{1,0,2:T(1,128)}, u32[]{:S(2)}) copy-start(s32[1,8,3]{1,0,2:T(1,128)} %param.14) | copy-start | bytes 292
  15.1 4.6 %copy-start.1 = (s32[1,14,3]{1,0,2:T(1,128)S(1)}, s32[1,14,3]{1,0,2:T(1,128)}, u32[]{:S(2)}) copy-start(s32[1,14,3]{1,0,2:T(1,128)} %param.17) | copy-start | bytes 508

commit v3 on v2

--- a/solution.py
+++ b/solution.py
@@ -68,8 +68,8 @@
     basis_hbm,
     transfer_hbm,
     coarse_hbm,
-    ahead,
-    behind,
+    inner,
+    outer,
     exchange,
     charges,
     basis,
@@ -86,17 +86,20 @@
     levels = leaves.bit_length() - 1
     position = lax.axis_index("leaf")
     body = lax.axis_index("top")
-    top_count = exchange.shape[1]
+    top_count = exchange.shape[0]
     width = 2 * points
     reach = NEAR * points // width
     whole = leaves // 2
     pairs = leaves - 1
     copies[0].wait()
     copies[1].wait()
+    odd = (position & 1) == 1
     for k in range(reach):
         first = (whole - reach + k) * width
-        ahead[pairs + k] = charges[0, :, first : first + width]
-        behind[pairs + k] = charges[0, :, k * width : (k + 1) * width]
+        high = charges[0, :, first : first + width]
+        low = charges[0, :, k * width : (k + 1) * width]
+        inner[pairs + k] = jnp.where(odd, low, high)
+        outer[pairs + k] = jnp.where(odd, high, low)
     copies[2].wait()
     product = path_product(coarse_transfer, position, coarse_transfer.shape[1])[-1]
     copies[3].wait()
@@ -105,8 +108,8 @@
         first, members = tier_span(leaves, height)
         for j in range(members // 2):
             pair = beside(coeffs[2 * j], coeffs[2 * j + 1])
-            ahead[first // 2 + j] = pair
-            behind[first // 2 + j] = pair
+            inner[first // 2 + j] = pair
+            outer[first // 2 + j] = pair
         coeffs = [
             mm(coeffs[2 * j], transfer[0, first + 2 * j])
             + mm(coeffs[2 * j + 1], transfer[0, first + 2 * j + 1])
@@ -116,7 +119,7 @@
     other = fold(mm(coeffs[0], product))
     for t in range(top_count):
         value = jnp.where(body == t, own, other)
-        exchange[:, t] = jnp.broadcast_to(value[None], (exchange.shape[0],) + value.shape)
+        exchange[t] = jnp.broadcast_to(value[None], (exchange.shape[1],) + value.shape)
 
 
 def prep_kernel(
@@ -143,7 +146,7 @@
         (coarse_coupling, opposite, body_coupling, near_blocks, coupling),
         sem,
     )
-    leaves, points, rank = basis.shape[1:]
+    leaves, _, rank = basis.shape[1:]
     levels = leaves.bit_length() - 1
     position = lax.axis_index("leaf")
     coarse = coarse_transfer.shape[1]
@@ -187,8 +190,8 @@
     coupling,
     local_path,
     mine,
-    below,
-    above,
+    from_inner,
+    from_outer,
     known,
     window,
     sources,
@@ -207,16 +210,18 @@
         ref[even] = jnp.where(low_lanes, pair, turned)
         ref[odd] = jnp.where(low_lanes, turned, pair)
 
+    odd = lax.axis_index("leaf") & 1
     for k in range(reach):
-        spread(below[pairs + k], sources, 2 * k, 2 * k + 1)
-        at = NEAR + leaves + 2 * k
-        spread(above[pairs + k], sources, at, at + 1)
+        at = (1 - odd) * (NEAR + leaves) + 2 * k
+        spread(from_inner[pairs + k], sources, at, at + 1)
+        at = odd * (NEAR + leaves) + 2 * k
+        spread(from_outer[pairs + k], sources, at, at + 1)
     for k in range(leaves // 2):
         at = NEAR + 2 * k
         spread(charges[0, :, k * width : (k + 1) * width], sources, at, at + 1)
     for height in range(levels):
         first, members = tier_span(leaves, height)
-        for block, pack in enumerate((below, mine, above)):
+        for block, pack in ((2 - 2 * odd, from_inner), (1, mine), (2 * odd, from_outer)):
             for j in range(members // 2):
                 at = 3 * first + block * members + 2 * j
                 spread(pack[first // 2 + j], window, at, at + 1)
@@ -243,22 +248,21 @@
 
 
 def final_kernel(received, known, mats, path, coarse_transfer, out, *tier_refs):
-    leaf_count, top_count = received.shape[0], received.shape[1]
+    top_count, leaf_count = received.shape[0], received.shape[1]
     coarse = coarse_transfer.shape[1]
-    rhs = out.shape[1]
     position = lax.axis_index("leaf")
     body = lax.axis_index("top")
     terms = []
     for s in range(top_count - 1):
         other = lax.rem(body + 1 + s, top_count)
-        total = received[0, other]
+        total = received[other, 0]
         for j in range(1, leaf_count):
-            total = total + received[j, other]
+            total = total + received[other, j]
         terms.append(unfold(total))
 
     def node(tier, index):
         if tier == 0:
-            return unfold(received[index, body])
+            return unfold(received[body, index])
         return tier_refs[tier - 1][index]
 
     for tier in range(coarse - 2):
@@ -315,12 +319,12 @@
     def stay(*arrays):
         return [pltpu.with_memory_space_constraint(array, HBM) for array in arrays]
 
-    ahead, behind, exchange, charges_v, basis_v, transfer_v, coarse_v = pl.pallas_call(
+    inner, outer, exchange, charges_v, basis_v, transfer_v, coarse_v = pl.pallas_call(
         up_kernel,
         out_shape=(
             pack_shape,
             pack_shape,
-            jax.ShapeDtypeStruct((leaf_count, top_count, rhs // 2, 2 * rank), f32),
+            jax.ShapeDtypeStruct((top_count, leaf_count, rhs // 2, 2 * rank), f32),
         )
         + like(charges, leaf_basis, local_transfer, coarse_transfer),
         in_specs=[hbm] * 4,
@@ -330,13 +334,13 @@
         compiler_params=params,
         cost_estimate=pl.CostEstimate(flops=40_000_000, bytes_accessed=1_000_000, transcendentals=0),
     )(*stay(charges, leaf_basis, local_transfer, coarse_transfer))
-    forward = [(i, (i + 1) % leaf_count) for i in range(leaf_count)]
-    backward = [(target, source) for source, target in forward]
-    below = lax.ppermute(ahead, "leaf", forward)
-    above = lax.ppermute(behind, "leaf", backward)
+    inner_pairs = [(i, i ^ 1) for i in range(leaf_count)]
+    outer_pairs = [(i, (i + (1 if i & 1 else -1)) % leaf_count) for i in range(leaf_count)]
+    from_inner = lax.ppermute(inner, "leaf", inner_pairs)
+    from_outer = lax.ppermute(outer, "leaf", outer_pairs)
     received = lax.all_to_all(
         exchange.reshape(leaf_count * top_count, rhs // 2, 2 * rank),
-        ("leaf", "top"),
+        ("top", "leaf"),
         0,
         0,
         tiled=True,
@@ -386,9 +390,9 @@
         near_v,
         coupling_v,
         local_path,
-        ahead,
-        below,
-        above,
+        inner,
+        from_inner,
+        from_outer,
     )
     return pl.pallas_call(
         final_kernel,

time: 23.2 us -> 23.1 us (level)
  waiting for transfers between devices: 1.67 us -> 1.23 us
  starting transfers between devices: 12.1 us -> 12.5 us
    ppermute x2, waiting for transfers between devices: 1.67 us -> 1.22 us  [the longest x1 1.22 us: per_device(): from_outer = lax.ppermute(outer, 'leaf', outer_pairs)]
    ppermute x2, starting transfers between devices: 4.78 us -> 5.15 us  [the longest x1 3.31 us: per_device(): from_outer = lax.ppermute(outer, 'leaf', outer_pairs)]
where the time goes in v3:
time: 23.1 us; the launch traced here: 22.9 us
  starting transfers between devices  12.5 us (54%)
  Pallas kernels  9.15 us (40%)
  waiting for transfers between devices  1.23 us (5%)
    all_to_all x1, starting transfers between devices, per_device(): lax.all_to_all(exchange.reshape(leaf_count * top_count, rhs // 2, 2 * ran...  7.34 us
    ppermute x1, starting transfers between devices, per_device(): from_outer = lax.ppermute(outer, 'leaf', outer_pairs)  3.31 us
    pallas_call x1, Pallas kernels, per_device(): pl.pallas_call(up_kernel, out_shape=(pack_shape, pack_shape, jax.ShapeDty...  2.95 us
    pallas_call x1, Pallas kernels, per_device(): pl.pallas_call(prep_kernel, out_shape=(jax.ShapeDtypeStruct((terms * rank...  2.92 us
    pallas_call x1, Pallas kernels, per_device(): pl.pallas_call(near_kernel, out_shape=jax.ShapeDtypeStruct((rhs, leaves *...  2.03 us
    ppermute x1, starting transfers between devices, per_device(): from_inner = lax.ppermute(inner, 'leaf', inner_pairs)  1.83 us
    pallas_call x1, Pallas kernels, per_device(): pl.pallas_call(final_kernel, out_shape=jax.ShapeDtypeStruct(charges.shape...  1.25 us
    ppermute x1, waiting for transfers between devices, per_device(): from_outer = lax.ppermute(outer, 'leaf', outer_pairs)  1.22 us
  transfers between devices with their start and end apart: 3, of which 1 were waited for; matrix products, arithmetic and copies ran while one was open for 0% of the time, Pallas kernels for 22%

profile of v3, /device:TPU:0, one launch (start us, length us, event | category | flops | bytes accessed | tf_op | source)
XLA Modules:
  0.0 22.9 jit_solution(10705347499933695034)
XLA Ops:
  0.0 2.9 %up.1 = (f32[9,16,128]{2,1,0:T(8,128)S(1)}, f32[9,16,128]{2,1,0:T(8,128)S(1)}, f32[4,8,8,128]{3,2,1,0:T(8,128)}, f32[1,16,512]{2,1,0:T(8,128)S(1)}, f32[1,8,64,6...) custom-call(f32[1,16,512]{2,1,0:T(8,128)} %charges_hbm.1, ...), custom_call_target="tpu_custom_call" | custom-call | flops 40000000 | bytes 1000000 | tf_op jit(solution)/shard_map/up/pallas_call | solution.py:322
  3.0 7.3 %all-to-all-start = ((f32[32,8,128]{2,1,0:T(8,128)}), f32[32,8,128]{2,1,0:T(8,128)S(1)}, u32[]{:S(2)}, u32[]{:S(2)}) async-start(f32[32,8,128]{2,1,0:T(8,128)} %bitcast), calls=%async_computation | async-start | bytes 262144 | tf_op jit(solution)/shard_map/all_to_all | solution.py:341
  10.3 1.8 %collective-permute-start = (f32[9,16,128]{2,1,0:T(8,128)S(1)}, f32[9,16,128]{2,1,0:T(8,128)S(1)}, u32[]{:S(2)}, u32[]{:S(2)}) collective-permute-start(f32[9,16,128]{2,1,0:T(8,128)S(1)} %get-tuple-element.25.mine), channel_id=1, source_target_pairs={{0,4},{4,0},{8,12},{12,8},{16,20},{20,16},{24,28},{28,24},{1,5},{5... | collective-permute-start | bytes 221192 | tf_op jit(solution)/shard_map/ppermute | solution.py:339
  12.1 3.3 %collective-permute-start.1 = (f32[9,16,128]{2,1,0:T(8,128)S(1)}, f32[9,16,128]{2,1,0:T(8,128)S(1)}, u32[]{:S(2)}, u32[]{:S(2)}) collective-permute-start(f32[9,16,128]{2,1,0:T(8,128)S(1)} %get-tuple-element.26), channel_id=1, source_target_pairs={{0,28},{4,8},{8,4},{12,16},{16,12},{20,24},{24,20},{28,0},{1,29},{... | collective-permute-start | bytes 221192 | tf_op jit(solution)/shard_map/ppermute | solution.py:340
  15.4 0.0 copy-start
  15.5 0.0 copy-start.1
  15.5 2.9 %prep.1 = (f32[512,64]{1,0:T(8,128)S(1)}, f32[8,192,64]{2,1,0:T(8,128)S(1)}, f32[8,64,64]{2,1,0:T(8,128)S(1)}, f32[1,8,3,64,64]{4,3,2,1,0:T(8,128)S(1)}, f32[1,14,3,64,64]{4,3,2,1,0:T(8,128)S(1)}) custom-call(f32[1,8,64,64]{3,2,1,0:T(8,128)S(1)} %get-tuple-element.19.basis, f32[1,14,64,64]{3,2,1,0:T(8,128)S(1)} %get-tuple-element.20.transfer, ...), custom_call_target="tpu_custom_call" | custom-call | flops 40000000 | bytes 2000000 | tf_op jit(solution)/shard_map/prep/pallas_call | solution.py:350
  18.4 0.0 collective-permute-done.from_inner
  18.4 1.2 %collective-permute-done.1.from_outer = f32[9,16,128]{2,1,0:T(8,128)S(1)} collective-permute-done((f32[9,16,128]{2,1,0:T(8,128)S(1)}, f32[9,16,128]{2,1,0:T(8,128)S(1)}, u32[]{:S(2)}, u32[]{:S(2)}) %collective-permute-start.1) | collective-permute-done | bytes 73760 | tf_op jit(solution)/shard_map/ppermute | solution.py:340
  19.6 0.0 copy-done
  19.6 0.0 copy-done.1
  19.6 2.0 %near.1.known = f32[16,512]{1,0:T(8,128)S(1)} custom-call(s32[3,1,8]{2,1,0:T(1,128)S(1)} %bitcast.5, s32[3,1,14]{2,1,0:T(1,128)S(1)} %bitcast.6, f32[1,16,512]{2,1,0:T(8,128)S(1)} %get-tuple-element.18.charges, f32[1,8,3,64,64]{4,3,2,1,0:T(8,128)S(1)} %get-tuple-element.22.near_blocks, f32[1,14,3,64,64]{4,3,2,1,0:T(8,128)S(1)} %get-tuple-element.23.coupling, ...), custom_call_target="tpu_custom_call" | custom-call | flops 80000000 | bytes 3000000 | tf_op jit(solution)/shard_map/near/pallas_call | solution.py:374
  21.6 0.0 all-to-all-done
  21.7 1.3 %final.1 = f32[1,16,512]{2,1,0:T(8,128)} custom-call(f32[4,8,8,128]{3,2,1,0:T(8,128)S(1)} %bitcast.4, f32[16,512]{1,0:T(8,128)S(1)} %near.1.known, f32[512,64]{1,0:T(8,128)S(1)} %get-tuple-element.27.mats, f32[8,64,64]{2,1,0:T(8,128)S(1)} %get-tuple-element.28.path, f32[1,3,2,64,64]{4,3,2,1,0:T(8,128)S(1)} %get-tuple-element.21.coarse_transfer), custom_call_target="tpu_custom_call" | custom-call | flops 10000000 | bytes 600000 | tf_op jit(solution)/shard_map/final/pallas_call | solution.py:397
Async XLA Ops:
  3.0 18.7 %all-to-all-start = ((f32[32,8,128]{2,1,0:T(8,128)}), f32[32,8,128]{2,1,0:T(8,128)S(1)}, u32[]{:S(2)}, u32[]{:S(2)}) async-start(f32[32,8,128]{2,1,0:T(8,128)} %bitcast), calls=%async_computation | async-start | bytes 262144 | tf_op jit(solution)/shard_map/all_to_all | solution.py:341
  10.3 8.1 %collective-permute-start = (f32[9,16,128]{2,1,0:T(8,128)S(1)}, f32[9,16,128]{2,1,0:T(8,128)S(1)}, u32[]{:S(2)}, u32[]{:S(2)}) collective-permute-start(f32[9,16,128]{2,1,0:T(8,128)S(1)} %get-tuple-element.25.mine), channel_id=1, source_target_pairs={{0,4},{4,0},{8,12},{12,8},{16,20},{20,16},{24,28},{28,24},{1,5},{5... | collective-permute-start | bytes 221192 | tf_op jit(solution)/shard_map/ppermute | solution.py:339
  12.1 7.5 %collective-permute-start.1 = (f32[9,16,128]{2,1,0:T(8,128)S(1)}, f32[9,16,128]{2,1,0:T(8,128)S(1)}, u32[]{:S(2)}, u32[]{:S(2)}) collective-permute-start(f32[9,16,128]{2,1,0:T(8,128)S(1)} %get-tuple-element.26), channel_id=1, source_target_pairs={{0,28},{4,8},{8,4},{12,16},{16,12},{20,24},{24,20},{28,0},{1,29},{... | collective-permute-start | bytes 221192 | tf_op jit(solution)/shard_map/ppermute | solution.py:340
  15.4 4.2 %copy-start = (s32[1,8,3]{1,0,2:T(1,128)S(1)}, s32[1,8,3]{1,0,2:T(1,128)}, u32[]{:S(2)}) copy-start(s32[1,8,3]{1,0,2:T(1,128)} %param.14) | copy-start | bytes 292
  15.5 4.2 %copy-start.1 = (s32[1,14,3]{1,0,2:T(1,128)S(1)}, s32[1,14,3]{1,0,2:T(1,128)}, u32[]{:S(2)}) copy-start(s32[1,14,3]{1,0,2:T(1,128)} %param.17) | copy-start | bytes 508

commit v4 on v3

--- a/solution.py
+++ b/solution.py
@@ -22,6 +22,37 @@
     return lax.dot_general(
         a, b, (((1,), (1,)), ((), ())), precision=HIGH, preferred_element_type=jnp.float32
     )
+
+
+def halves(x):
+    high = x.astype(jnp.bfloat16)
+    return high, (x - high.astype(jnp.float32)).astype(jnp.bfloat16)
+
+
+def packed(x):
+    high = x.astype(jnp.bfloat16).astype(jnp.float32)
+    return beside(high, x - high).astype(jnp.bfloat16)
+
+
+def stacked(x):
+    high, low = halves(x)
+    return jnp.concatenate([high, low], axis=0)
+
+
+def mm_s(a, b):
+    rows = a.shape[0]
+    left = stacked(a)
+    high, low = halves(b)
+    value = dot(left, high)
+    return value[:rhs_of(value)] + value[rhs_of(value):] + dot(left[:rows], low)
+
+
+def rhs_of(value):
+    return value.shape[0] // 2
+
+
+def dot(a, b):
+    return lax.dot_general(a, b, (((1,), (0,)), ((), ())), preferred_element_type=jnp.float32)
 
 
 def beside(a, b):
@@ -68,6 +99,7 @@
     basis_hbm,
     transfer_hbm,
     coarse_hbm,
+    coupling_hbm,
     inner,
     outer,
     exchange,
@@ -75,11 +107,12 @@
     basis,
     transfer,
     coarse_transfer,
+    coupling,
     sem,
 ):
     copies = fetch(
-        (charges_hbm, basis_hbm, coarse_hbm, transfer_hbm),
-        (charges, basis, coarse_transfer, transfer),
+        (charges_hbm, basis_hbm, coarse_hbm, transfer_hbm, coupling_hbm),
+        (charges, basis, coarse_transfer, transfer, coupling),
         sem,
     )
     leaves, points = basis.shape[1], basis.shape[2]
@@ -100,70 +133,87 @@
         low = charges[0, :, k * width : (k + 1) * width]
         inner[pairs + k] = jnp.where(odd, low, high)
         outer[pairs + k] = jnp.where(odd, high, low)
+    coeffs = [mm_s(charges[0, :, g * points : (g + 1) * points], basis[0, g]) for g in range(leaves)]
     copies[2].wait()
-    product = path_product(coarse_transfer, position, coarse_transfer.shape[1])[-1]
     copies[3].wait()
-    coeffs = [mm(charges[0, :, g * points : (g + 1) * points], basis[0, g]) for g in range(leaves)]
+    tiers = coarse_transfer.shape[1]
+    first, members = tier_span(leaves, levels - 1)
+    steps = [coarse_transfer[0, tier, (position >> tier) & 1] for tier in range(tiers)]
+    ends = [mm(transfer[0, first + n], steps[0]) for n in range(members)]
+    rest = None
+    for step in steps[:0:-1]:
+        rest = step if rest is None else mm(step, rest)
+    ends = [mm(end, rest) for end in ends]
     for height in range(levels):
         first, members = tier_span(leaves, height)
         for j in range(members // 2):
             pair = beside(coeffs[2 * j], coeffs[2 * j + 1])
             inner[first // 2 + j] = pair
             outer[first // 2 + j] = pair
+        below = coeffs
         coeffs = [
-            mm(coeffs[2 * j], transfer[0, first + 2 * j])
-            + mm(coeffs[2 * j + 1], transfer[0, first + 2 * j + 1])
+            mm_s(below[2 * j], transfer[0, first + 2 * j])
+            + mm_s(below[2 * j + 1], transfer[0, first + 2 * j + 1])
             for j in range(members // 2)
         ]
     own = fold(coeffs[0])
-    other = fold(mm(coeffs[0], product))
+    other = fold(mm_s(below[0], ends[0]) + mm_s(below[1], ends[1]))
     for t in range(top_count):
         value = jnp.where(body == t, own, other)
         exchange[t] = jnp.broadcast_to(value[None], (exchange.shape[1],) + value.shape)
+    copies[4].wait()
 
 
 def prep_kernel(
     basis,
     transfer,
     coarse_transfer,
+    coupling,
     coarse_coupling_hbm,
     opposite_hbm,
     body_coupling_hbm,
     near_hbm,
-    coupling_hbm,
     mats,
+    path,
     local_path,
-    path,
-    near_blocks,
-    coupling,
+    near_pack,
+    coupling_pack,
     coarse_coupling,
     opposite,
     body_coupling,
+    near_blocks,
     sem,
 ):
     copies = fetch(
-        (coarse_coupling_hbm, opposite_hbm, body_coupling_hbm, near_hbm, coupling_hbm),
-        (coarse_coupling, opposite, body_coupling, near_blocks, coupling),
+        (coarse_coupling_hbm, opposite_hbm, body_coupling_hbm, near_hbm),
+        (coarse_coupling, opposite, body_coupling, near_blocks),
         sem,
     )
-    leaves, _, rank = basis.shape[1:]
+    leaves, points, rank = basis.shape[1:]
     levels = leaves.bit_length() - 1
     position = lax.axis_index("leaf")
     coarse = coarse_transfer.shape[1]
+    ends = []
     for g in range(leaves):
         product = basis[0, g]
         for height in range(levels):
-            local_path[g, height * rank : (height + 1) * rank] = product.T
+            local_path[g, height * rank : (height + 1) * rank] = packed(product.T)
             first, _ = tier_span(leaves, height)
             product = mm(product, transfer[0, first + (g >> height)])
-        path[g] = product.T
+        ends.append(product.T)
+    for j in range(leaves // 2):
+        columns = slice(2 * j * points, 2 * (j + 1) * points)
+        path[0, :, columns], path[1, :, columns] = halves(beside(ends[2 * j], ends[2 * j + 1]))
+    for n in range(2 * leaves - 2):
+        coupling_pack[n] = packed(coupling[0, n].reshape(3 * rank, rank))
 
     products = path_product(coarse_transfer, position, coarse)
     at = 0
 
     def put(value):
         nonlocal at
-        mats[at : at + rank] = value
+        rows = slice(at, at + rank)
+        mats[0, rows], mats[1, rows] = halves(value)
         at += rank
 
     for copy in copies[:3]:
@@ -178,16 +228,17 @@
     far = mm_t(opposite[0], products[coarse - 3])
     put(mm(coarse_transfer[0, coarse - 3, 0], far))
     put(mm(coarse_transfer[0, coarse - 3, 1], far))
-    for copy in copies[3:]:
-        copy.wait()
+    copies[3].wait()
+    for g in range(leaves):
+        near_pack[g] = packed(near_blocks[0, g].reshape(3 * points, points))
 
 
 def near_kernel(
     near_list,
     coupling_list,
     charges,
-    near_blocks,
-    coupling,
+    near_pack,
+    coupling_pack,
     local_path,
     mine,
     from_inner,
@@ -196,8 +247,8 @@
     window,
     sources,
 ):
-    leaves, points = near_blocks.shape[1], near_blocks.shape[3]
-    rank = coupling.shape[3]
+    leaves = near_pack.shape[0]
+    points = near_pack.shape[2] // 2
     rhs = charges.shape[1]
     levels = leaves.bit_length() - 1
     pairs = leaves - 1
@@ -210,46 +261,66 @@
         ref[even] = jnp.where(low_lanes, pair, turned)
         ref[odd] = jnp.where(low_lanes, turned, pair)
 
-    odd = lax.axis_index("leaf") & 1
+    parity = lax.axis_index("leaf") & 1
     for k in range(reach):
-        at = (1 - odd) * (NEAR + leaves) + 2 * k
+        at = (1 - parity) * (NEAR + leaves) + 2 * k
         spread(from_inner[pairs + k], sources, at, at + 1)
-        at = odd * (NEAR + leaves) + 2 * k
+        at = parity * (NEAR + leaves) + 2 * k
         spread(from_outer[pairs + k], sources, at, at + 1)
     for k in range(leaves // 2):
         at = NEAR + 2 * k
         spread(charges[0, :, k * width : (k + 1) * width], sources, at, at + 1)
     for height in range(levels):
         first, members = tier_span(leaves, height)
-        for block, pack in ((2 - 2 * odd, from_inner), (1, mine), (2 * odd, from_outer)):
-            for j in range(members // 2):
-                at = 3 * first + block * members + 2 * j
-                spread(pack[first // 2 + j], window, at, at + 1)
-
-    def three(ref, base, list_ref, n):
-        a = ref[base + list_ref[0, 0, n]]
-        b = ref[base + list_ref[1, 0, n]]
-        c = ref[base + list_ref[2, 0, n]]
+        for j in range(members // 2):
+            k = first // 2 + j
+            at = 3 * first + 2 * j
+            spread(from_inner[k], window, at + (2 - 2 * parity) * members, at + (2 - 2 * parity) * members + 1)
+            spread(mine[k], window, at + members, at + members + 1)
+            spread(
+                from_outer[k],
+                window,
+                at + 2 * parity * members,
+                at + 2 * parity * members + 1,
+            )
+
+    def three(a, b, c):
         return beside(jnp.where(low_lanes, a, b), c[:, :points])
+
+    def picked(ref, base, list_ref, n):
+        return three(*(ref[base + list_ref[slot, 0, n]] for slot in range(3)))
+
+    def product(left, weights):
+        value = dot(stacked(left), weights)
+        return value[:rhs] + jnp.where(low_lanes, value[rhs:], 0.0)
+
+    def folded(value):
+        return value + pltpu.roll(value, points, 1)
 
     coupled = []
     for n in range(2 * leaves - 2):
         height = next(h for h in range(levels) if n < sum(tier_span(leaves, h)))
-        left = three(window, 3 * tier_span(leaves, height)[0], coupling_list, n)
-        coupled.append(mm(left, coupling[0, n].reshape(3 * rank, rank)))
+        left = picked(window, 3 * tier_span(leaves, height)[0], coupling_list, n)
+        coupled.append(folded(product(left, coupling_pack[n])))
     result = []
     for g in range(leaves):
-        left = three(sources, g, near_list, g)
-        value = mm(left, near_blocks[0, g].reshape(3 * points, points))
+        value = product(picked(sources, g, near_list, g), near_pack[g])
         chain = [coupled[tier_span(leaves, h)[0] + (g >> h)] for h in range(levels)]
-        result.append(value + mm(jnp.concatenate(chain, axis=1), local_path[g]))
+        left = [
+            jnp.where(low_lanes, chain[h], chain[h + 1]) if h + 1 < levels else chain[h][:, :points]
+            for h in range(0, levels, 2)
+        ]
+        result.append(folded(value + product(jnp.concatenate(left, axis=1), local_path[g])))
     for j in range(leaves // 2):
-        known[:, j * width : (j + 1) * width] = beside(result[2 * j], result[2 * j + 1])
+        known[:, j * width : (j + 1) * width] = jnp.where(
+            low_lanes, result[2 * j], result[2 * j + 1]
+        )
 
 
 def final_kernel(received, known, mats, path, coarse_transfer, out, *tier_refs):
     top_count, leaf_count = received.shape[0], received.shape[1]
     coarse = coarse_transfer.shape[1]
+    rhs = out.shape[1]
     position = lax.axis_index("leaf")
     body = lax.axis_index("top")
     terms = []
@@ -279,12 +350,11 @@
     across = ((position >> (coarse - 2)) + 2) & 3
     terms.append(node(coarse - 3, 2 * across))
     terms.append(node(coarse - 3, 2 * across + 1))
-    local = mm(jnp.concatenate(terms, axis=1), mats[...])
-    points = path.shape[2]
-    for j in range(path.shape[0] // 2):
-        at = 2 * j * points
-        value = beside(mm(local, path[2 * j]), mm(local, path[2 * j + 1]))
-        out[0, :, at : at + 2 * points] = known[:, at : at + 2 * points] + value
+    left = stacked(jnp.concatenate(terms, axis=1))
+    value = dot(left, mats[0])
+    left = stacked(value[:rhs] + value[rhs:] + dot(left[:rhs], mats[1]))
+    value = dot(left, path[0])
+    out[0] = known[...] + value[:rhs] + value[rhs:] + dot(left[:rhs], path[1])
 
 
 def per_device(
@@ -319,21 +389,23 @@
     def stay(*arrays):
         return [pltpu.with_memory_space_constraint(array, HBM) for array in arrays]
 
-    inner, outer, exchange, charges_v, basis_v, transfer_v, coarse_v = pl.pallas_call(
+    inner, outer, exchange, charges_v, basis_v, transfer_v, coarse_v, coupling_v = pl.pallas_call(
         up_kernel,
         out_shape=(
             pack_shape,
             pack_shape,
             jax.ShapeDtypeStruct((top_count, leaf_count, rhs // 2, 2 * rank), f32),
         )
-        + like(charges, leaf_basis, local_transfer, coarse_transfer),
-        in_specs=[hbm] * 4,
-        out_specs=(vmem,) * 7,
-        scratch_shapes=[pltpu.SemaphoreType.DMA((4,))],
+        + like(charges, leaf_basis, local_transfer, coarse_transfer, local_coupling),
+        in_specs=[hbm] * 5,
+        out_specs=(vmem,) * 8,
+        scratch_shapes=[pltpu.SemaphoreType.DMA((5,))],
         name="up",
         compiler_params=params,
         cost_estimate=pl.CostEstimate(flops=40_000_000, bytes_accessed=1_000_000, transcendentals=0),
-    )(*stay(charges, leaf_basis, local_transfer, coarse_transfer))
+    )(
+        *stay(charges, leaf_basis, local_transfer, coarse_transfer, local_coupling)
+    )
     inner_pairs = [(i, i ^ 1) for i in range(leaf_count)]
     outer_pairs = [(i, (i + (1 if i & 1 else -1)) % leaf_count) for i in range(leaf_count)]
     from_inner = lax.ppermute(inner, "leaf", inner_pairs)
@@ -347,21 +419,23 @@
     ).reshape(exchange.shape)
     terms = (top_count - 1) + 3 * (coarse - 2) + 2
     levels = leaves.bit_length() - 1
-    mats, local_path, path, near_v, coupling_v = pl.pallas_call(
+    bf16 = jnp.bfloat16
+    mats, path, local_path, near_pack, coupling_pack = pl.pallas_call(
         prep_kernel,
         out_shape=(
-            jax.ShapeDtypeStruct((terms * rank, rank), f32),
-            jax.ShapeDtypeStruct((leaves, levels * rank, points), f32),
-            jax.ShapeDtypeStruct((leaves, rank, points), f32),
-        )
-        + like(near_blocks, local_coupling),
-        in_specs=[vmem] * 3 + [hbm] * 5,
+            jax.ShapeDtypeStruct((2, terms * rank, rank), bf16),
+            jax.ShapeDtypeStruct((2, rank, leaves * points), bf16),
+            jax.ShapeDtypeStruct((leaves, levels * rank, 2 * points), bf16),
+            jax.ShapeDtypeStruct((leaves, 3 * points, 2 * points), bf16),
+            jax.ShapeDtypeStruct((2 * leaves - 2, 3 * rank, 2 * rank), bf16),
+        ),
+        in_specs=[vmem] * 4 + [hbm] * 4,
         out_specs=(vmem,) * 5,
         scratch_shapes=[
             pltpu.VMEM(array.shape, f32)
-            for array in (coarse_coupling, opposite_coupling, body_coupling)
+            for array in (coarse_coupling, opposite_coupling, body_coupling, near_blocks)
         ]
-        + [pltpu.SemaphoreType.DMA((5,))],
+        + [pltpu.SemaphoreType.DMA((4,))],
         name="prep",
         compiler_params=params,
         cost_estimate=pl.CostEstimate(flops=40_000_000, bytes_accessed=2_000_000, transcendentals=0),
@@ -369,7 +443,8 @@
         basis_v,
         transfer_v,
         coarse_v,
-        *stay(coarse_coupling, opposite_coupling, body_coupling, near_blocks, local_coupling),
+        coupling_v,
+        *stay(coarse_coupling, opposite_coupling, body_coupling, near_blocks),
     )
     known = pl.pallas_call(
         near_kernel,
@@ -387,8 +462,8 @@
         jnp.transpose(near_list, (2, 0, 1)),
         jnp.transpose(coupling_list, (2, 0, 1)),
         charges_v,
-        near_v,
-        coupling_v,
+        near_pack,
+        coupling_pack,
         local_path,
         inner,
         from_inner,

time: 23.1 us -> 22.1 us (0.957)
  Pallas kernels: 9.15 us -> 8.4 us
  waiting for transfers between devices: 1.23 us -> 0.98 us
    pallas_call x1, Pallas kernels: 2.03 us -> 1.51 us  [per_device(): pl.pallas_call(near_kernel, out_shape=jax.ShapeDtypeStruct((rhs, leaves *...]
    pallas_call x1, Pallas kernels: 2.95 us -> 2.68 us  [per_device(): pl.pallas_call(up_kernel, out_shape=(pack_shape, pack_shape, jax.ShapeDty...]
    ppermute x1, waiting for transfers between devices: 1.22 us -> 0.97 us  [per_device(): from_outer = lax.ppermute(outer, 'leaf', outer_pairs)]
    pallas_call x1, Pallas kernels: 2.92 us -> 3.16 us  [per_device(): pl.pallas_call(prep_kernel, out_shape=(jax.ShapeDtypeStruct((2, terms * r...]
  transfers between devices with their start and end apart: 3 -> 3, of which waited for: 1 -> 1; matrix products, arithmetic and copies ran while one was open for 0% -> 0% of each run, Pallas kernels for 22% -> 21%
where the time goes in v4:
time: 22.1 us; the launch traced here: 21.9 us
  starting transfers between devices  12.5 us (57%)
  Pallas kernels  8.4 us (38%)
  waiting for transfers between devices  0.98 us (4%)
    all_to_all x1, starting transfers between devices, per_device(): lax.all_to_all(exchange.reshape(leaf_count * top_count, rhs // 2, 2 * ran...  7.33 us
    ppermute x1, starting transfers between devices, per_device(): from_outer = lax.ppermute(outer, 'leaf', outer_pairs)  3.31 us
    pallas_call x1, Pallas kernels, per_device(): pl.pallas_call(prep_kernel, out_shape=(jax.ShapeDtypeStruct((2, terms * r...  3.16 us
    pallas_call x1, Pallas kernels, per_device(): pl.pallas_call(up_kernel, out_shape=(pack_shape, pack_shape, jax.ShapeDty...  2.68 us
    ppermute x1, starting transfers between devices, per_device(): from_inner = lax.ppermute(inner, 'leaf', inner_pairs)  1.83 us
    pallas_call x1, Pallas kernels, per_device(): pl.pallas_call(near_kernel, out_shape=jax.ShapeDtypeStruct((rhs, leaves *...  1.51 us
    pallas_call x1, Pallas kernels, per_device(): pl.pallas_call(final_kernel, out_shape=jax.ShapeDtypeStruct(charges.shape...  1.05 us
    ppermute x1, waiting for transfers between devices, per_device(): from_outer = lax.ppermute(outer, 'leaf', outer_pairs)  0.97 us
  transfers between devices with their start and end apart: 3, of which 1 were waited for; matrix products, arithmetic and copies ran while one was open for 0% of the time, Pallas kernels for 21%

profile of v4, /device:TPU:0, one launch (start us, length us, event | category | flops | bytes accessed | tf_op | source)
XLA Modules:
  0.0 21.9 jit_solution(13479127624228202756)
XLA Ops:
  0.0 2.7 %up.1 = (f32[9,16,128]{2,1,0:T(8,128)S(1)}, f32[9,16,128]{2,1,0:T(8,128)S(1)}, f32[4,8,8,128]{3,2,1,0:T(8,128)}, f32[1,16,512]{2,1,0:T(8,128)S(1)}, f32[1,8,64,6...) custom-call(f32[1,16,512]{2,1,0:T(8,128)} %charges_hbm.1, ...), custom_call_target="tpu_custom_call" | custom-call | flops 40000000 | bytes 1000000 | tf_op jit(solution)/shard_map/up/pallas_call | solution.py:392
  2.7 7.3 %all-to-all-start = ((f32[32,8,128]{2,1,0:T(8,128)}), f32[32,8,128]{2,1,0:T(8,128)S(1)}, u32[]{:S(2)}, u32[]{:S(2)}) async-start(f32[32,8,128]{2,1,0:T(8,128)} %bitcast), calls=%async_computation | async-start | bytes 262144 | tf_op jit(solution)/shard_map/all_to_all | solution.py:413
  10.0 1.8 %collective-permute-start = (f32[9,16,128]{2,1,0:T(8,128)S(1)}, f32[9,16,128]{2,1,0:T(8,128)S(1)}, u32[]{:S(2)}, u32[]{:S(2)}) collective-permute-start(f32[9,16,128]{2,1,0:T(8,128)S(1)} %get-tuple-element.27.mine), channel_id=1, source_target_pairs={{0,4},{4,0},{8,12},{12,8},{16,20},{20,16},{24,28},{28,24},{1,5},{5... | collective-permute-start | bytes 221192 | tf_op jit(solution)/shard_map/ppermute | solution.py:411
  11.9 3.3 %collective-permute-start.1 = (f32[9,16,128]{2,1,0:T(8,128)S(1)}, f32[9,16,128]{2,1,0:T(8,128)S(1)}, u32[]{:S(2)}, u32[]{:S(2)}) collective-permute-start(f32[9,16,128]{2,1,0:T(8,128)S(1)} %get-tuple-element.28), channel_id=1, source_target_pairs={{0,28},{4,8},{8,4},{12,16},{16,12},{20,24},{24,20},{28,0},{1,29},{... | collective-permute-start | bytes 221192 | tf_op jit(solution)/shard_map/ppermute | solution.py:412
  15.2 0.0 copy-start
  15.2 0.0 copy-start.1
  15.2 3.2 %prep.1 = (bf16[2,512,64]{2,1,0:T(8,128)(2,1)S(1)}, bf16[2,64,512]{2,1,0:T(8,128)(2,1)S(1)}, bf16[8,192,128]{2,1,0:T(8,128)(2,1)S(1)}, bf16[8,192,128]{2,1,0:T(8,128)(2,1)S(1)}, bf16[14,192,128]{2,1,0:T(8,128)(2,1)S(1)}) custom-call(f32[1,8,64,64]{3,2,1,0:T(8,128)S(1)} %get-tuple-element.20.basis, f32[1,14,64,64]{3,2,1,0:T(8,128)S(1)} %get-tuple-element.21.transfer, ...), custom_call_target="tpu_custom_call" | custom-call | flops 40000000 | bytes 2000000 | tf_op jit(solution)/shard_map/prep/pallas_call | solution.py:423
  18.3 0.0 collective-permute-done.from_inner
  18.4 1.0 %collective-permute-done.1.from_outer = f32[9,16,128]{2,1,0:T(8,128)S(1)} collective-permute-done((f32[9,16,128]{2,1,0:T(8,128)S(1)}, f32[9,16,128]{2,1,0:T(8,128)S(1)}, u32[]{:S(2)}, u32[]{:S(2)}) %collective-permute-start.1) | collective-permute-done | bytes 73760 | tf_op jit(solution)/shard_map/ppermute | solution.py:412
  19.3 0.0 copy-done
  19.3 0.0 copy-done.1
  19.3 1.5 %near.1.known = f32[16,512]{1,0:T(8,128)S(1)} custom-call(s32[3,1,8]{2,1,0:T(1,128)S(1)} %bitcast.5, s32[3,1,14]{2,1,0:T(1,128)S(1)} %bitcast.6, f32[1,16,512]{2,1,0:T(8,128)S(1)} %get-tuple-element.19.charges, bf16[8,192,128]{2,1,0:T(8,128)(2,1)S(1)} %get-tuple-element.24.near_pack, bf16[14,192,128]{2,1,0:T(8,128)(2,1)S(1)} %get-tuple-element.25.coupling_pack, ...), custom_call_target="tpu_custom_call" | custom-call | flops 80000000 | bytes 3000000 | tf_op jit(solution)/shard_map/near/pallas_call | solution.py:449
  20.8 0.0 all-to-all-done
  20.9 1.1 %final.1 = f32[1,16,512]{2,1,0:T(8,128)} custom-call(f32[4,8,8,128]{3,2,1,0:T(8,128)S(1)} %bitcast.4, f32[16,512]{1,0:T(8,128)S(1)} %near.1.known, bf16[2,512,64]{2,1,0:T(8,128)(2,1)S(1)} %get-tuple-element.29.mats, bf16[2,64,512]{2,1,0:T(8,128)(2,1)S(1)} %get-tuple-element.30.path, f32[1,3,2,64,64]{4,3,2,1,0:T(8,128)S(1)} %get-tuple-element.22.coarse_transfer), custom_call_target="tpu_custom_call" | custom-call | flops 10000000 | bytes 600000 | tf_op jit(solution)/shard_map/final/pallas_call | solution.py:472
Async XLA Ops:
  2.7 18.2 %all-to-all-start = ((f32[32,8,128]{2,1,0:T(8,128)}), f32[32,8,128]{2,1,0:T(8,128)S(1)}, u32[]{:S(2)}, u32[]{:S(2)}) async-start(f32[32,8,128]{2,1,0:T(8,128)} %bitcast), calls=%async_computation | async-start | bytes 262144 | tf_op jit(solution)/shard_map/all_to_all | solution.py:413
  10.0 8.3 %collective-permute-start = (f32[9,16,128]{2,1,0:T(8,128)S(1)}, f32[9,16,128]{2,1,0:T(8,128)S(1)}, u32[]{:S(2)}, u32[]{:S(2)}) collective-permute-start(f32[9,16,128]{2,1,0:T(8,128)S(1)} %get-tuple-element.27.mine), channel_id=1, source_target_pairs={{0,4},{4,0},{8,12},{12,8},{16,20},{20,16},{24,28},{28,24},{1,5},{5... | collective-permute-start | bytes 221192 | tf_op jit(solution)/shard_map/ppermute | solution.py:411
  11.9 7.5 %collective-permute-start.1 = (f32[9,16,128]{2,1,0:T(8,128)S(1)}, f32[9,16,128]{2,1,0:T(8,128)S(1)}, u32[]{:S(2)}, u32[]{:S(2)}) collective-permute-start(f32[9,16,128]{2,1,0:T(8,128)S(1)} %get-tuple-element.28), channel_id=1, source_target_pairs={{0,28},{4,8},{8,4},{12,16},{16,12},{20,24},{24,20},{28,0},{1,29},{... | collective-permute-start | bytes 221192 | tf_op jit(solution)/shard_map/ppermute | solution.py:412
  15.2 4.2 %copy-start = (s32[1,8,3]{1,0,2:T(1,128)S(1)}, s32[1,8,3]{1,0,2:T(1,128)}, u32[]{:S(2)}) copy-start(s32[1,8,3]{1,0,2:T(1,128)} %param.14) | copy-start | bytes 292
  15.2 4.2 %copy-start.1 = (s32[1,14,3]{1,0,2:T(1,128)S(1)}, s32[1,14,3]{1,0,2:T(1,128)}, u32[]{:S(2)}) copy-start(s32[1,14,3]{1,0,2:T(1,128)} %param.17) | copy-start | bytes 508

commit v5 on v4

--- a/solution.py
+++ b/solution.py
@@ -100,8 +100,8 @@
     transfer_hbm,
     coarse_hbm,
     coupling_hbm,
-    inner,
-    outer,
+    ahead,
+    behind,
     exchange,
     charges,
     basis,
@@ -126,13 +126,12 @@
     pairs = leaves - 1
     copies[0].wait()
     copies[1].wait()
-    odd = (position & 1) == 1
     for k in range(reach):
         first = (whole - reach + k) * width
         high = charges[0, :, first : first + width]
         low = charges[0, :, k * width : (k + 1) * width]
-        inner[pairs + k] = jnp.where(odd, low, high)
-        outer[pairs + k] = jnp.where(odd, high, low)
+        ahead[pairs + k] = high
+        behind[pairs + k] = low
     coeffs = [mm_s(charges[0, :, g * points : (g + 1) * points], basis[0, g]) for g in range(leaves)]
     copies[2].wait()
     copies[3].wait()
@@ -148,8 +147,8 @@
         first, members = tier_span(leaves, height)
         for j in range(members // 2):
             pair = beside(coeffs[2 * j], coeffs[2 * j + 1])
-            inner[first // 2 + j] = pair
-            outer[first // 2 + j] = pair
+            ahead[first // 2 + j] = pair
+            behind[first // 2 + j] = pair
         below = coeffs
         coeffs = [
             mm_s(below[2 * j], transfer[0, first + 2 * j])
@@ -164,6 +163,35 @@
     copies[4].wait()
 
 
+def paths(basis, transfer, path, leaf_path, pair_path):
+    leaves, points, rank = basis.shape[1:]
+    levels = leaves.bit_length() - 1
+    flipped = [basis[0, g].T for g in range(leaves)]
+    for g in range(leaves):
+        leaf_path[g] = packed(flipped[g])
+    wide = [
+        beside(*(mm_s(transfer[0, g].T, flipped[g]) for g in (2 * j, 2 * j + 1)))
+        for j in range(leaves // 2)
+    ]
+    width = 2 * points
+    for height in range(1, levels):
+        first, members = tier_span(leaves, height)
+        for j in range(leaves // 2):
+            group = leaves // 2 // len(wide)
+            at = (j % group) * width
+            rows = slice((height - 1) * rank, height * rank)
+            pair_path[j, rows, :width], pair_path[j, rows, width:] = halves(
+                wide[j // group][:, at : at + width]
+            )
+        if len(wide) > members:
+            wide = [beside(wide[2 * n], wide[2 * n + 1]) for n in range(members)]
+        wide = [mm_s(transfer[0, first + n].T, wide[n]) for n in range(members)]
+    for n in range(len(wide)):
+        size = leaves * points // len(wide)
+        columns = slice(n * size, (n + 1) * size)
+        path[0, :, columns], path[1, :, columns] = halves(wide[n])
+
+
 def prep_kernel(
     basis,
     transfer,
@@ -173,9 +201,10 @@
     opposite_hbm,
     body_coupling_hbm,
     near_hbm,
+    path,
+    leaf_path,
+    pair_path,
     mats,
-    path,
-    local_path,
     near_pack,
     coupling_pack,
     coarse_coupling,
@@ -189,24 +218,17 @@
         (coarse_coupling, opposite, body_coupling, near_blocks),
         sem,
     )
+    position = lax.axis_index("leaf")
+
+
+    @pl.when(position >= 0)
+    def _():
+        paths(basis, transfer, path, leaf_path, pair_path)
+
     leaves, points, rank = basis.shape[1:]
-    levels = leaves.bit_length() - 1
-    position = lax.axis_index("leaf")
     coarse = coarse_transfer.shape[1]
-    ends = []
-    for g in range(leaves):
-        product = basis[0, g]
-        for height in range(levels):
-            local_path[g, height * rank : (height + 1) * rank] = packed(product.T)
-            first, _ = tier_span(leaves, height)
-            product = mm(product, transfer[0, first + (g >> height)])
-        ends.append(product.T)
-    for j in range(leaves // 2):
-        columns = slice(2 * j * points, 2 * (j + 1) * points)
-        path[0, :, columns], path[1, :, columns] = halves(beside(ends[2 * j], ends[2 * j + 1]))
     for n in range(2 * leaves - 2):
         coupling_pack[n] = packed(coupling[0, n].reshape(3 * rank, rank))
-
     products = path_product(coarse_transfer, position, coarse)
     at = 0
 
@@ -239,10 +261,11 @@
     charges,
     near_pack,
     coupling_pack,
-    local_path,
+    leaf_path,
+    pair_path,
     mine,
-    from_inner,
-    from_outer,
+    below,
+    above,
     known,
     window,
     sources,
@@ -261,28 +284,19 @@
         ref[even] = jnp.where(low_lanes, pair, turned)
         ref[odd] = jnp.where(low_lanes, turned, pair)
 
-    parity = lax.axis_index("leaf") & 1
     for k in range(reach):
-        at = (1 - parity) * (NEAR + leaves) + 2 * k
-        spread(from_inner[pairs + k], sources, at, at + 1)
-        at = parity * (NEAR + leaves) + 2 * k
-        spread(from_outer[pairs + k], sources, at, at + 1)
+        spread(below[pairs + k], sources, 2 * k, 2 * k + 1)
+        at = NEAR + leaves + 2 * k
+        spread(above[pairs + k], sources, at, at + 1)
     for k in range(leaves // 2):
         at = NEAR + 2 * k
         spread(charges[0, :, k * width : (k + 1) * width], sources, at, at + 1)
     for height in range(levels):
         first, members = tier_span(leaves, height)
-        for j in range(members // 2):
-            k = first // 2 + j
-            at = 3 * first + 2 * j
-            spread(from_inner[k], window, at + (2 - 2 * parity) * members, at + (2 - 2 * parity) * members + 1)
-            spread(mine[k], window, at + members, at + members + 1)
-            spread(
-                from_outer[k],
-                window,
-                at + 2 * parity * members,
-                at + 2 * parity * members + 1,
-            )
+        for block, pack in enumerate((below, mine, above)):
+            for j in range(members // 2):
+                at = 3 * first + block * members + 2 * j
+                spread(pack[first // 2 + j], window, at, at + 1)
 
     def three(a, b, c):
         return beside(jnp.where(low_lanes, a, b), c[:, :points])
@@ -305,14 +319,16 @@
     result = []
     for g in range(leaves):
         value = product(picked(sources, g, near_list, g), near_pack[g])
-        chain = [coupled[tier_span(leaves, h)[0] + (g >> h)] for h in range(levels)]
+        result.append(folded(value + product(coupled[g][:, :points], leaf_path[g])))
+    for j in range(leaves // 2):
+        chain = [coupled[tier_span(leaves, h)[0] + (2 * j >> h)] for h in range(1, levels)]
         left = [
-            jnp.where(low_lanes, chain[h], chain[h + 1]) if h + 1 < levels else chain[h][:, :points]
-            for h in range(0, levels, 2)
+            jnp.where(low_lanes, *chain[h : h + 2]) if h + 1 < len(chain) else chain[h][:, :points]
+            for h in range(0, len(chain), 2)
         ]
-        result.append(folded(value + product(jnp.concatenate(left, axis=1), local_path[g])))
-    for j in range(leaves // 2):
-        known[:, j * width : (j + 1) * width] = jnp.where(
+        value = dot(stacked(jnp.concatenate(left, axis=1)), pair_path[j])
+        value = value[:rhs, :width] + value[:rhs, width:] + value[rhs:, :width]
+        known[:, j * width : (j + 1) * width] = value + jnp.where(
             low_lanes, result[2 * j], result[2 * j + 1]
         )
 
@@ -389,7 +405,7 @@
     def stay(*arrays):
         return [pltpu.with_memory_space_constraint(array, HBM) for array in arrays]
 
-    inner, outer, exchange, charges_v, basis_v, transfer_v, coarse_v, coupling_v = pl.pallas_call(
+    ahead, behind, exchange, charges_v, basis_v, transfer_v, coarse_v, coupling_v = pl.pallas_call(
         up_kernel,
         out_shape=(
             pack_shape,
@@ -406,10 +422,10 @@
     )(
         *stay(charges, leaf_basis, local_transfer, coarse_transfer, local_coupling)
     )
-    inner_pairs = [(i, i ^ 1) for i in range(leaf_count)]
-    outer_pairs = [(i, (i + (1 if i & 1 else -1)) % leaf_count) for i in range(leaf_count)]
-    from_inner = lax.ppermute(inner, "leaf", inner_pairs)
-    from_outer = lax.ppermute(outer, "leaf", outer_pairs)
+    forward = [(i, (i + 1) % leaf_count) for i in range(leaf_count)]
+    backward = [(target, source) for source, target in forward]
+    below = lax.ppermute(ahead, "leaf", forward)
+    above = lax.ppermute(behind, "leaf", backward)
     received = lax.all_to_all(
         exchange.reshape(leaf_count * top_count, rhs // 2, 2 * rank),
         ("top", "leaf"),
@@ -420,17 +436,18 @@
     terms = (top_count - 1) + 3 * (coarse - 2) + 2
     levels = leaves.bit_length() - 1
     bf16 = jnp.bfloat16
-    mats, path, local_path, near_pack, coupling_pack = pl.pallas_call(
+    path, leaf_path, pair_path, mats, near_pack, coupling_pack = pl.pallas_call(
         prep_kernel,
         out_shape=(
+            jax.ShapeDtypeStruct((2, rank, leaves * points), bf16),
+            jax.ShapeDtypeStruct((leaves, rank, 2 * points), bf16),
+            jax.ShapeDtypeStruct((leaves // 2, (levels - 1) * rank, 4 * points), bf16),
             jax.ShapeDtypeStruct((2, terms * rank, rank), bf16),
-            jax.ShapeDtypeStruct((2, rank, leaves * points), bf16),
-            jax.ShapeDtypeStruct((leaves, levels * rank, 2 * points), bf16),
             jax.ShapeDtypeStruct((leaves, 3 * points, 2 * points), bf16),
             jax.ShapeDtypeStruct((2 * leaves - 2, 3 * rank, 2 * rank), bf16),
         ),
         in_specs=[vmem] * 4 + [hbm] * 4,
-        out_specs=(vmem,) * 5,
+        out_specs=(vmem,) * 6,
         scratch_shapes=[
             pltpu.VMEM(array.shape, f32)
             for array in (coarse_coupling, opposite_coupling, body_coupling, near_blocks)
@@ -438,7 +455,7 @@
         + [pltpu.SemaphoreType.DMA((4,))],
         name="prep",
         compiler_params=params,
-        cost_estimate=pl.CostEstimate(flops=40_000_000, bytes_accessed=2_000_000, transcendentals=0),
+        cost_estimate=pl.CostEstimate(flops=20_000_000, bytes_accessed=2_000_000, transcendentals=0),
     )(
         basis_v,
         transfer_v,
@@ -449,7 +466,7 @@
     known = pl.pallas_call(
         near_kernel,
         out_shape=jax.ShapeDtypeStruct((rhs, leaves * points), f32),
-        in_specs=[smem] * 2 + [vmem] * 7,
+        in_specs=[smem] * 2 + [vmem] * 8,
         out_specs=vmem,
         scratch_shapes=[
             pltpu.VMEM((3 * (2 * leaves - 2), rhs, 2 * rank), f32),
@@ -464,10 +481,11 @@
         charges_v,
         near_pack,
         coupling_pack,
-        local_path,
-        inner,
-        from_inner,
-        from_outer,
+        leaf_path,
+        pair_path,
+        ahead,
+        below,
+        above,
     )
     return pl.pallas_call(
         final_kernel,

time: 22.1 us -> 21.9 us (level)
  waiting for transfers between devices: 0.98 us -> 2.83 us
  Pallas kernels: 8.4 us -> 6.74 us
  starting transfers between devices: 12.5 us -> 12.1 us
    ppermute x2, waiting for transfers between devices: 0.98 us -> 2.83 us  [the longest x1 2.82 us: per_device(): below = lax.ppermute(ahead, 'leaf', forward)]
    pallas_call x1, Pallas kernels: 3.16 us -> 1.69 us  [per_device(): pl.pallas_call(prep_kernel, out_shape=(jax.ShapeDtypeStruct((2, rank, lea...]
    ppermute x2, starting transfers between devices: 5.15 us -> 4.78 us  [the longest x1 2.95 us: per_device(): above = lax.ppermute(behind, 'leaf', backward)]
  transfers between devices with their start and end apart: 3 -> 3, of which waited for: 1 -> 1; matrix products, arithmetic and copies ran while one was open for 0% -> 0% of each run, Pallas kernels for 21% -> 14%
where the time goes in v5:
time: 21.9 us; the launch traced here: 21.7 us
  starting transfers between devices  12.1 us (55%)
  Pallas kernels  6.74 us (31%)
  waiting for transfers between devices  2.83 us (13%)
    all_to_all x1, starting transfers between devices, per_device(): lax.all_to_all(exchange.reshape(leaf_count * top_count, rhs // 2, 2 * ran...  7.33 us
    ppermute x1, starting transfers between devices, per_device(): above = lax.ppermute(behind, 'leaf', backward)  2.95 us
    ppermute x1, waiting for transfers between devices, per_device(): below = lax.ppermute(ahead, 'leaf', forward)  2.82 us
    pallas_call x1, Pallas kernels, per_device(): pl.pallas_call(up_kernel, out_shape=(pack_shape, pack_shape, jax.ShapeDty...  2.68 us
    ppermute x1, starting transfers between devices, per_device(): below = lax.ppermute(ahead, 'leaf', forward)  1.82 us
    pallas_call x1, Pallas kernels, per_device(): pl.pallas_call(prep_kernel, out_shape=(jax.ShapeDtypeStruct((2, rank, lea...  1.69 us
    pallas_call x1, Pallas kernels, per_device(): pl.pallas_call(near_kernel, out_shape=jax.ShapeDtypeStruct((rhs, leaves *...  1.32 us
    pallas_call x1, Pallas kernels, per_device(): pl.pallas_call(final_kernel, out_shape=jax.ShapeDtypeStruct(charges.shape...  1.05 us
  transfers between devices with their start and end apart: 3, of which 1 were waited for; matrix products, arithmetic and copies ran while one was open for 0% of the time, Pallas kernels for 14%

profile of v5, /device:TPU:0, one launch (start us, length us, event | category | flops | bytes accessed | tf_op | source)
XLA Modules:
  0.0 21.7 jit_solution(10402678807918846465)
XLA Ops:
  0.0 2.7 %up.1 = (f32[9,16,128]{2,1,0:T(8,128)S(1)}, f32[9,16,128]{2,1,0:T(8,128)S(1)}, f32[4,8,8,128]{3,2,1,0:T(8,128)}, f32[1,16,512]{2,1,0:T(8,128)S(1)}, f32[1,8,64,6...) custom-call(f32[1,16,512]{2,1,0:T(8,128)} %charges_hbm.1, ...), custom_call_target="tpu_custom_call" | custom-call | flops 40000000 | bytes 1000000 | tf_op jit(solution)/shard_map/up/pallas_call | solution.py:408
  2.7 7.3 %all-to-all-start = ((f32[32,8,128]{2,1,0:T(8,128)}), f32[32,8,128]{2,1,0:T(8,128)S(1)}, u32[]{:S(2)}, u32[]{:S(2)}) async-start(f32[32,8,128]{2,1,0:T(8,128)} %bitcast), calls=%async_computation | async-start | bytes 262144 | tf_op jit(solution)/shard_map/all_to_all | solution.py:429
  10.0 1.8 %collective-permute-start = (f32[9,16,128]{2,1,0:T(8,128)S(1)}, f32[9,16,128]{2,1,0:T(8,128)S(1)}, u32[]{:S(2)}, u32[]{:S(2)}) collective-permute-start(f32[9,16,128]{2,1,0:T(8,128)S(1)} %get-tuple-element.29.mine), channel_id=1, source_target_pairs={{0,4},{4,8},{8,12},{12,16},{16,20},{20,24},{24,28},{28,0},{1,5},{5... | collective-permute-start | bytes 221192 | tf_op jit(solution)/shard_map/ppermute | solution.py:427
  11.8 3.0 %collective-permute-start.1 = (f32[9,16,128]{2,1,0:T(8,128)S(1)}, f32[9,16,128]{2,1,0:T(8,128)S(1)}, u32[]{:S(2)}, u32[]{:S(2)}) collective-permute-start(f32[9,16,128]{2,1,0:T(8,128)S(1)} %get-tuple-element.30), channel_id=1, source_target_pairs={{4,0},{8,4},{12,8},{16,12},{20,16},{24,20},{28,24},{0,28},{5,1},{9... | collective-permute-start | bytes 221192 | tf_op jit(solution)/shard_map/ppermute | solution.py:428
  14.8 0.0 copy-start
  14.8 0.0 copy-start.1
  14.8 1.7 %prep.1 = (bf16[2,64,512]{2,1,0:T(8,128)(2,1)S(1)}, bf16[8,64,128]{2,1,0:T(8,128)(2,1)S(1)}, bf16[4,128,256]{2,1,0:T(8,128)(2,1)S(1)}, bf16[2,512,64]{2,1,0:T(8,...) custom-call(f32[1,8,64,64]{3,2,1,0:T(8,128)S(1)} %get-tuple-element.21.basis, ...), custom_call_target="tpu_custom_call" | custom-call | flops 20000000 | bytes 2000000 | tf_op jit(solution)/shard_map/prep/pallas_call | solution.py:439
  16.5 2.8 %collective-permute-done.below = f32[9,16,128]{2,1,0:T(8,128)S(1)} collective-permute-done((f32[9,16,128]{2,1,0:T(8,128)S(1)}, f32[9,16,128]{2,1,0:T(8,128)S(1)}, u32[]{:S(2)}, u32[]{:S(2)}) %collective-permute-start) | collective-permute-done | bytes 73760 | tf_op jit(solution)/shard_map/ppermute | solution.py:427
  19.3 0.0 collective-permute-done.1.above
  19.3 0.0 copy-done
  19.3 0.0 copy-done.1
  19.3 1.3 %near.1.known = f32[16,512]{1,0:T(8,128)S(1)} custom-call(s32[3,1,8]{2,1,0:T(1,128)S(1)} %bitcast.5, s32[3,1,14]{2,1,0:T(1,128)S(1)} %bitcast.6, f32[1,16,512]{2,1,0:T(8,128)S(1)} %get-tuple-element.20.charges, bf16[8,192,128]{2,1,0:T(8,128)(2,1)S(1)} %get-tuple-element.25.near_pack, bf16[14,192,128]{2,1,0:T(8,128)(2,1)S(1)} %get-tuple-element.26.coupling_pack, ...), custom_call_target="tpu_custom_call" | custom-call | flops 80000000 | bytes 3000000 | tf_op jit(solution)/shard_map/near/pallas_call | solution.py:466
  20.7 0.0 all-to-all-done
  20.7 1.1 %final.1 = f32[1,16,512]{2,1,0:T(8,128)} custom-call(f32[4,8,8,128]{3,2,1,0:T(8,128)S(1)} %bitcast.4, f32[16,512]{1,0:T(8,128)S(1)} %near.1.known, bf16[2,512,64]{2,1,0:T(8,128)(2,1)S(1)} %get-tuple-element.31.mats, bf16[2,64,512]{2,1,0:T(8,128)(2,1)S(1)} %get-tuple-element.32.path, f32[1,3,2,64,64]{4,3,2,1,0:T(8,128)S(1)} %get-tuple-element.23.coarse_transfer), custom_call_target="tpu_custom_call" | custom-call | flops 10000000 | bytes 600000 | tf_op jit(solution)/shard_map/final/pallas_call | solution.py:490
Async XLA Ops:
  2.7 18.0 %all-to-all-start = ((f32[32,8,128]{2,1,0:T(8,128)}), f32[32,8,128]{2,1,0:T(8,128)S(1)}, u32[]{:S(2)}, u32[]{:S(2)}) async-start(f32[32,8,128]{2,1,0:T(8,128)} %bitcast), calls=%async_computation | async-start | bytes 262144 | tf_op jit(solution)/shard_map/all_to_all | solution.py:429
  10.0 9.3 %collective-permute-start = (f32[9,16,128]{2,1,0:T(8,128)S(1)}, f32[9,16,128]{2,1,0:T(8,128)S(1)}, u32[]{:S(2)}, u32[]{:S(2)}) collective-permute-start(f32[9,16,128]{2,1,0:T(8,128)S(1)} %get-tuple-element.29.mine), channel_id=1, source_target_pairs={{0,4},{4,8},{8,12},{12,16},{16,20},{20,24},{24,28},{28,0},{1,5},{5... | collective-permute-start | bytes 221192 | tf_op jit(solution)/shard_map/ppermute | solution.py:427
  11.8 7.5 %collective-permute-start.1 = (f32[9,16,128]{2,1,0:T(8,128)S(1)}, f32[9,16,128]{2,1,0:T(8,128)S(1)}, u32[]{:S(2)}, u32[]{:S(2)}) collective-permute-start(f32[9,16,128]{2,1,0:T(8,128)S(1)} %get-tuple-element.30), channel_id=1, source_target_pairs={{4,0},{8,4},{12,8},{16,12},{20,16},{24,20},{28,24},{0,28},{5,1},{9... | collective-permute-start | bytes 221192 | tf_op jit(solution)/shard_map/ppermute | solution.py:428
  14.8 4.5 %copy-start = (s32[1,8,3]{1,0,2:T(1,128)S(1)}, s32[1,8,3]{1,0,2:T(1,128)}, u32[]{:S(2)}) copy-start(s32[1,8,3]{1,0,2:T(1,128)} %param.14) | copy-start | bytes 292
  14.8 4.5 %copy-start.1 = (s32[1,14,3]{1,0,2:T(1,128)S(1)}, s32[1,14,3]{1,0,2:T(1,128)}, u32[]{:S(2)}) copy-start(s32[1,14,3]{1,0,2:T(1,128)} %param.17) | copy-start | bytes 508

commit v6 on v5

--- a/solution.py
+++ b/solution.py
@@ -57,11 +57,6 @@
 
 def beside(a, b):
     return jnp.concatenate([a, b], axis=1)
-
-
-def fold(x):
-    half = x.shape[0] // 2
-    return beside(x[:half], x[half:])
 
 
 def unfold(x):
@@ -132,31 +127,47 @@
         low = charges[0, :, k * width : (k + 1) * width]
         ahead[pairs + k] = high
         behind[pairs + k] = low
-    coeffs = [mm_s(charges[0, :, g * points : (g + 1) * points], basis[0, g]) for g in range(leaves)]
+    rhs = charges.shape[1]
+    low_lanes = lax.broadcasted_iota(jnp.int32, (rhs, width), 1) < points
+    coeffs = []
+    for j in range(whole):
+        pair = charges[0, :, j * width : (j + 1) * width]
+        left = jnp.concatenate(
+            [jnp.where(low_lanes, pair, 0.0), jnp.where(low_lanes, 0.0, pair)], axis=0
+        )
+        value = mm_s(left, basis[0, 2 * j : 2 * j + 2].reshape(width, basis.shape[3]))
+        coeffs += [value[:rhs], value[rhs:]]
     copies[2].wait()
     copies[3].wait()
     tiers = coarse_transfer.shape[1]
     first, members = tier_span(leaves, levels - 1)
     steps = [coarse_transfer[0, tier, (position >> tier) & 1] for tier in range(tiers)]
-    ends = [mm(transfer[0, first + n], steps[0]) for n in range(members)]
-    rest = None
-    for step in steps[:0:-1]:
-        rest = step if rest is None else mm(step, rest)
-    ends = [mm(end, rest) for end in ends]
+    ends = [mm_s(transfer[0, first + n], steps[0]) for n in range(members)]
+    rest = beside(steps[-1], steps[-1])
+    for step in steps[-2:0:-1]:
+        rest = mm_s(step, rest)
+    ends = [mm_s(end, rest) for end in ends]
+    tops = [beside(transfer[0, first + n], transfer[0, first + n]) for n in range(members)]
     for height in range(levels):
         first, members = tier_span(leaves, height)
         for j in range(members // 2):
             pair = beside(coeffs[2 * j], coeffs[2 * j + 1])
             ahead[first // 2 + j] = pair
             behind[first // 2 + j] = pair
-        below = coeffs
-        coeffs = [
-            mm_s(below[2 * j], transfer[0, first + 2 * j])
-            + mm_s(below[2 * j + 1], transfer[0, first + 2 * j + 1])
-            for j in range(members // 2)
-        ]
-    own = fold(coeffs[0])
-    other = fold(mm_s(below[0], ends[0]) + mm_s(below[1], ends[1]))
+        if height < levels - 1:
+            coeffs = [
+                mm_s(coeffs[2 * j], transfer[0, first + 2 * j])
+                + mm_s(coeffs[2 * j + 1], transfer[0, first + 2 * j + 1])
+                for j in range(members // 2)
+            ]
+    half = rhs // 2
+
+    def doubled(weights):
+        value = mm_s(coeffs[0], weights[0]) + mm_s(coeffs[1], weights[1])
+        return jnp.where(low_lanes[:half], value[:half], value[half:])
+
+    own = doubled(tops)
+    other = doubled(ends)
     for t in range(top_count):
         value = jnp.where(body == t, own, other)
         exchange[t] = jnp.broadcast_to(value[None], (exchange.shape[1],) + value.shape)
@@ -319,7 +330,7 @@
     result = []
     for g in range(leaves):
         value = product(picked(sources, g, near_list, g), near_pack[g])
-        result.append(folded(value + product(coupled[g][:, :points], leaf_path[g])))
+        result.append(value + product(coupled[g][:, :points], leaf_path[g]))
     for j in range(leaves // 2):
         chain = [coupled[tier_span(leaves, h)[0] + (2 * j >> h)] for h in range(1, levels)]
         left = [
@@ -328,8 +339,10 @@
         ]
         value = dot(stacked(jnp.concatenate(left, axis=1)), pair_path[j])
         value = value[:rhs, :width] + value[:rhs, width:] + value[rhs:, :width]
-        known[:, j * width : (j + 1) * width] = value + jnp.where(
-            low_lanes, result[2 * j], result[2 * j + 1]
+        even, odd = result[2 * j], result[2 * j + 1]
+        value = value + jnp.where(low_lanes, even, odd)
+        known[:, j * width : (j + 1) * width] = value + pltpu.roll(
+            jnp.where(low_lanes, odd, even), points, 1
         )
 
 

time: 21.9 us -> 21.9 us (level)
  no operation moved by 1% of the time
where the time goes in v6:
time: 21.9 us; the launch traced here: 21.7 us
  starting transfers between devices  12.1 us (55%)
  Pallas kernels  6.71 us (31%)
  waiting for transfers between devices  2.82 us (13%)
    all_to_all x1, starting transfers between devices, per_device(): lax.all_to_all(exchange.reshape(leaf_count * top_count, rhs // 2, 2 * ran...  7.33 us
    ppermute x1, starting transfers between devices, per_device(): above = lax.ppermute(behind, 'leaf', backward)  2.95 us
    ppermute x1, waiting for transfers between devices, per_device(): below = lax.ppermute(ahead, 'leaf', forward)  2.82 us
    pallas_call x1, Pallas kernels, per_device(): pl.pallas_call(up_kernel, out_shape=(pack_shape, pack_shape, jax.ShapeDty...  2.64 us
    ppermute x1, starting transfers between devices, per_device(): below = lax.ppermute(ahead, 'leaf', forward)  1.82 us
    pallas_call x1, Pallas kernels, per_device(): pl.pallas_call(prep_kernel, out_shape=(jax.ShapeDtypeStruct((2, rank, lea...  1.7 us
    pallas_call x1, Pallas kernels, per_device(): pl.pallas_call(near_kernel, out_shape=jax.ShapeDtypeStruct((rhs, leaves *...  1.31 us
    pallas_call x1, Pallas kernels, per_device(): pl.pallas_call(final_kernel, out_shape=jax.ShapeDtypeStruct(charges.shape...  1.06 us
  transfers between devices with their start and end apart: 3, of which 1 were waited for; matrix products, arithmetic and copies ran while one was open for 0% of the time, Pallas kernels for 14%

profile of v6, /device:TPU:0, one launch (start us, length us, event | category | flops | bytes accessed | tf_op | source)
XLA Modules:
  0.0 21.7 jit_solution(3998186776940086215)
XLA Ops:
  0.0 2.6 %up.1 = (f32[9,16,128]{2,1,0:T(8,128)S(1)}, f32[9,16,128]{2,1,0:T(8,128)S(1)}, f32[4,8,8,128]{3,2,1,0:T(8,128)}, f32[1,16,512]{2,1,0:T(8,128)S(1)}, f32[1,8,64,6...) custom-call(f32[1,16,512]{2,1,0:T(8,128)} %charges_hbm.1, ...), custom_call_target="tpu_custom_call" | custom-call | flops 40000000 | bytes 1000000 | tf_op jit(solution)/shard_map/up/pallas_call | solution.py:421
  2.6 7.3 %all-to-all-start = ((f32[32,8,128]{2,1,0:T(8,128)}), f32[32,8,128]{2,1,0:T(8,128)S(1)}, u32[]{:S(2)}, u32[]{:S(2)}) async-start(f32[32,8,128]{2,1,0:T(8,128)} %bitcast), calls=%async_computation | async-start | bytes 262144 | tf_op jit(solution)/shard_map/all_to_all | solution.py:442
  10.0 1.8 %collective-permute-start = (f32[9,16,128]{2,1,0:T(8,128)S(1)}, f32[9,16,128]{2,1,0:T(8,128)S(1)}, u32[]{:S(2)}, u32[]{:S(2)}) collective-permute-start(f32[9,16,128]{2,1,0:T(8,128)S(1)} %get-tuple-element.29.mine), channel_id=1, source_target_pairs={{0,4},{4,8},{8,12},{12,16},{16,20},{20,24},{24,28},{28,0},{1,5},{5... | collective-permute-start | bytes 221192 | tf_op jit(solution)/shard_map/ppermute | solution.py:440
  11.8 3.0 %collective-permute-start.1 = (f32[9,16,128]{2,1,0:T(8,128)S(1)}, f32[9,16,128]{2,1,0:T(8,128)S(1)}, u32[]{:S(2)}, u32[]{:S(2)}) collective-permute-start(f32[9,16,128]{2,1,0:T(8,128)S(1)} %get-tuple-element.30), channel_id=1, source_target_pairs={{4,0},{8,4},{12,8},{16,12},{20,16},{24,20},{28,24},{0,28},{5,1},{9... | collective-permute-start | bytes 221192 | tf_op jit(solution)/shard_map/ppermute | solution.py:441
  14.8 0.0 copy-start
  14.8 0.0 copy-start.1
  14.8 1.7 %prep.1 = (bf16[2,64,512]{2,1,0:T(8,128)(2,1)S(1)}, bf16[8,64,128]{2,1,0:T(8,128)(2,1)S(1)}, bf16[4,128,256]{2,1,0:T(8,128)(2,1)S(1)}, bf16[2,512,64]{2,1,0:T(8,...) custom-call(f32[1,8,64,64]{3,2,1,0:T(8,128)S(1)} %get-tuple-element.21.basis, ...), custom_call_target="tpu_custom_call" | custom-call | flops 20000000 | bytes 2000000 | tf_op jit(solution)/shard_map/prep/pallas_call | solution.py:452
  16.5 2.8 %collective-permute-done.below = f32[9,16,128]{2,1,0:T(8,128)S(1)} collective-permute-done((f32[9,16,128]{2,1,0:T(8,128)S(1)}, f32[9,16,128]{2,1,0:T(8,128)S(1)}, u32[]{:S(2)}, u32[]{:S(2)}) %collective-permute-start) | collective-permute-done | bytes 73760 | tf_op jit(solution)/shard_map/ppermute | solution.py:440
  19.3 0.0 collective-permute-done.1.above
  19.3 0.0 copy-done
  19.3 0.0 copy-done.1
  19.3 1.3 %near.1.known = f32[16,512]{1,0:T(8,128)S(1)} custom-call(s32[3,1,8]{2,1,0:T(1,128)S(1)} %bitcast.5, s32[3,1,14]{2,1,0:T(1,128)S(1)} %bitcast.6, f32[1,16,512]{2,1,0:T(8,128)S(1)} %get-tuple-element.20.charges, bf16[8,192,128]{2,1,0:T(8,128)(2,1)S(1)} %get-tuple-element.25.near_pack, bf16[14,192,128]{2,1,0:T(8,128)(2,1)S(1)} %get-tuple-element.26.coupling_pack, ...), custom_call_target="tpu_custom_call" | custom-call | flops 80000000 | bytes 3000000 | tf_op jit(solution)/shard_map/near/pallas_call | solution.py:479
  20.6 0.0 all-to-all-done
  20.6 1.1 %final.1 = f32[1,16,512]{2,1,0:T(8,128)} custom-call(f32[4,8,8,128]{3,2,1,0:T(8,128)S(1)} %bitcast.4, f32[16,512]{1,0:T(8,128)S(1)} %near.1.known, bf16[2,512,64]{2,1,0:T(8,128)(2,1)S(1)} %get-tuple-element.31.mats, bf16[2,64,512]{2,1,0:T(8,128)(2,1)S(1)} %get-tuple-element.32.path, f32[1,3,2,64,64]{4,3,2,1,0:T(8,128)S(1)} %get-tuple-element.23.coarse_transfer), custom_call_target="tpu_custom_call" | custom-call | flops 10000000 | bytes 600000 | tf_op jit(solution)/shard_map/final/pallas_call | solution.py:503
Async XLA Ops:
  2.6 18.0 %all-to-all-start = ((f32[32,8,128]{2,1,0:T(8,128)}), f32[32,8,128]{2,1,0:T(8,128)S(1)}, u32[]{:S(2)}, u32[]{:S(2)}) async-start(f32[32,8,128]{2,1,0:T(8,128)} %bitcast), calls=%async_computation | async-start | bytes 262144 | tf_op jit(solution)/shard_map/all_to_all | solution.py:442
  10.0 9.3 %collective-permute-start = (f32[9,16,128]{2,1,0:T(8,128)S(1)}, f32[9,16,128]{2,1,0:T(8,128)S(1)}, u32[]{:S(2)}, u32[]{:S(2)}) collective-permute-start(f32[9,16,128]{2,1,0:T(8,128)S(1)} %get-tuple-element.29.mine), channel_id=1, source_target_pairs={{0,4},{4,8},{8,12},{12,16},{16,20},{20,24},{24,28},{28,0},{1,5},{5... | collective-permute-start | bytes 221192 | tf_op jit(solution)/shard_map/ppermute | solution.py:440
  11.8 7.5 %collective-permute-start.1 = (f32[9,16,128]{2,1,0:T(8,128)S(1)}, f32[9,16,128]{2,1,0:T(8,128)S(1)}, u32[]{:S(2)}, u32[]{:S(2)}) collective-permute-start(f32[9,16,128]{2,1,0:T(8,128)S(1)} %get-tuple-element.30), channel_id=1, source_target_pairs={{4,0},{8,4},{12,8},{16,12},{20,16},{24,20},{28,24},{0,28},{5,1},{9... | collective-permute-start | bytes 221192 | tf_op jit(solution)/shard_map/ppermute | solution.py:441
  14.8 4.5 %copy-start = (s32[1,8,3]{1,0,2:T(1,128)S(1)}, s32[1,8,3]{1,0,2:T(1,128)}, u32[]{:S(2)}) copy-start(s32[1,8,3]{1,0,2:T(1,128)} %param.14) | copy-start | bytes 292
  14.8 4.5 %copy-start.1 = (s32[1,14,3]{1,0,2:T(1,128)S(1)}, s32[1,14,3]{1,0,2:T(1,128)}, u32[]{:S(2)}) copy-start(s32[1,14,3]{1,0,2:T(1,128)} %param.17) | copy-start | bytes 508

commit v7 on v6

--- a/solution.py
+++ b/solution.py
@@ -8,7 +8,6 @@
 NEAR = 4
 HIGH = lax.Precision.HIGH
 VMEM = pltpu.MemorySpace.VMEM
-SMEM = pltpu.MemorySpace.SMEM
 HBM = pltpu.MemorySpace.HBM
 
 
@@ -267,8 +266,8 @@
 
 
 def near_kernel(
-    near_list,
-    coupling_list,
+    near_list_in,
+    coupling_list_in,
     charges,
     near_pack,
     coupling_pack,
@@ -280,7 +279,11 @@
     known,
     window,
     sources,
+    near_list,
+    coupling_list,
+    sem,
 ):
+    copies = fetch((near_list_in, coupling_list_in), (near_list, coupling_list), sem)
     leaves = near_pack.shape[0]
     points = near_pack.shape[2] // 2
     rhs = charges.shape[1]
@@ -308,6 +311,9 @@
             for j in range(members // 2):
                 at = 3 * first + block * members + 2 * j
                 spread(pack[first // 2 + j], window, at, at + 1)
+
+    for copy in copies:
+        copy.wait()
 
     def three(a, b, c):
         return beside(jnp.where(low_lanes, a, b), c[:, :points])
@@ -407,7 +413,6 @@
     packs = leaves - 1 + NEAR // 2
     f32 = jnp.float32
     vmem = pl.BlockSpec(memory_space=VMEM)
-    smem = pl.BlockSpec(memory_space=SMEM)
     params = pltpu.CompilerParams(vmem_limit_bytes=8 << 20)
     pack_shape = jax.ShapeDtypeStruct((packs, rhs, 2 * rank), f32)
     hbm = pl.BlockSpec(memory_space=HBM)
@@ -479,11 +484,14 @@
     known = pl.pallas_call(
         near_kernel,
         out_shape=jax.ShapeDtypeStruct((rhs, leaves * points), f32),
-        in_specs=[smem] * 2 + [vmem] * 8,
+        in_specs=[vmem] * 10,
         out_specs=vmem,
         scratch_shapes=[
             pltpu.VMEM((3 * (2 * leaves - 2), rhs, 2 * rank), f32),
             pltpu.VMEM((leaves + 2 * NEAR, rhs, 2 * points), f32),
+            pltpu.SMEM((near_list.shape[2], 1, leaves), jnp.int32),
+            pltpu.SMEM((coupling_list.shape[2], 1, 2 * leaves - 2), jnp.int32),
+            pltpu.SemaphoreType.DMA((2,)),
         ],
         name="near",
         compiler_params=params,

time: 21.9 us -> 21.8 us (level)
  no operation moved by 1% of the time
where the time goes in v7:
time: 21.8 us; the launch traced here: 21.6 us
  starting transfers between devices  12.1 us (56%)
  Pallas kernels  6.64 us (30%)
  waiting for transfers between devices  2.82 us (13%)
    all_to_all x1, starting transfers between devices, per_device(): lax.all_to_all(exchange.reshape(leaf_count * top_count, rhs // 2, 2 * ran...  7.33 us
    ppermute x1, starting transfers between devices, per_device(): above = lax.ppermute(behind, 'leaf', backward)  2.95 us
    ppermute x1, waiting for transfers between devices, per_device(): below = lax.ppermute(ahead, 'leaf', forward)  2.82 us
    pallas_call x1, Pallas kernels, per_device(): pl.pallas_call(up_kernel, out_shape=(pack_shape, pack_shape, jax.ShapeDty...  2.64 us
    ppermute x1, starting transfers between devices, per_device(): below = lax.ppermute(ahead, 'leaf', forward)  1.82 us
    pallas_call x1, Pallas kernels, per_device(): pl.pallas_call(prep_kernel, out_shape=(jax.ShapeDtypeStruct((2, rank, lea...  1.7 us
    pallas_call x1, Pallas kernels, per_device(): pl.pallas_call(near_kernel, out_shape=jax.ShapeDtypeStruct((rhs, leaves *...  1.25 us
    pallas_call x1, Pallas kernels, per_device(): pl.pallas_call(final_kernel, out_shape=jax.ShapeDtypeStruct(charges.shape...  1.05 us
  transfers between devices with their start and end apart: 3, of which 1 were waited for; matrix products, arithmetic and copies ran while one was open for 0% of the time, Pallas kernels for 14%

profile of v7, /device:TPU:0, one launch (start us, length us, event | category | flops | bytes accessed | tf_op | source)
XLA Modules:
  0.0 21.6 jit_solution(17568321291751624830)
XLA Ops:
  0.0 2.6 %up.1 = (f32[9,16,128]{2,1,0:T(8,128)S(1)}, f32[9,16,128]{2,1,0:T(8,128)S(1)}, f32[4,8,8,128]{3,2,1,0:T(8,128)}, f32[1,16,512]{2,1,0:T(8,128)S(1)}, f32[1,8,64,6...) custom-call(f32[1,16,512]{2,1,0:T(8,128)} %charges_hbm.1, ...), custom_call_target="tpu_custom_call" | custom-call | flops 40000000 | bytes 1000000 | tf_op jit(solution)/shard_map/up/pallas_call | solution.py:426
  2.6 7.3 %all-to-all-start = ((f32[32,8,128]{2,1,0:T(8,128)}), f32[32,8,128]{2,1,0:T(8,128)S(1)}, u32[]{:S(2)}, u32[]{:S(2)}) async-start(f32[32,8,128]{2,1,0:T(8,128)} %bitcast), calls=%async_computation | async-start | bytes 262144 | tf_op jit(solution)/shard_map/all_to_all | solution.py:447
  10.0 1.8 %collective-permute-start = (f32[9,16,128]{2,1,0:T(8,128)S(1)}, f32[9,16,128]{2,1,0:T(8,128)S(1)}, u32[]{:S(2)}, u32[]{:S(2)}) collective-permute-start(f32[9,16,128]{2,1,0:T(8,128)S(1)} %get-tuple-element.29.mine), channel_id=1, source_target_pairs={{0,4},{4,8},{8,12},{12,16},{16,20},{20,24},{24,28},{28,0},{1,5},{5... | collective-permute-start | bytes 221192 | tf_op jit(solution)/shard_map/ppermute | solution.py:445
  11.8 3.0 %collective-permute-start.1 = (f32[9,16,128]{2,1,0:T(8,128)S(1)}, f32[9,16,128]{2,1,0:T(8,128)S(1)}, u32[]{:S(2)}, u32[]{:S(2)}) collective-permute-start(f32[9,16,128]{2,1,0:T(8,128)S(1)} %get-tuple-element.30), channel_id=1, source_target_pairs={{4,0},{8,4},{12,8},{16,12},{20,16},{24,20},{28,24},{0,28},{5,1},{9... | collective-permute-start | bytes 221192 | tf_op jit(solution)/shard_map/ppermute | solution.py:446
  14.8 0.0 copy-start
  14.8 0.0 copy-start.1
  14.8 1.7 %prep.1 = (bf16[2,64,512]{2,1,0:T(8,128)(2,1)S(1)}, bf16[8,64,128]{2,1,0:T(8,128)(2,1)S(1)}, bf16[4,128,256]{2,1,0:T(8,128)(2,1)S(1)}, bf16[2,512,64]{2,1,0:T(8,...) custom-call(f32[1,8,64,64]{3,2,1,0:T(8,128)S(1)} %get-tuple-element.21.basis, ...), custom_call_target="tpu_custom_call" | custom-call | flops 20000000 | bytes 2000000 | tf_op jit(solution)/shard_map/prep/pallas_call | solution.py:457
  16.5 2.8 %collective-permute-done.below = f32[9,16,128]{2,1,0:T(8,128)S(1)} collective-permute-done((f32[9,16,128]{2,1,0:T(8,128)S(1)}, f32[9,16,128]{2,1,0:T(8,128)S(1)}, u32[]{:S(2)}, u32[]{:S(2)}) %collective-permute-start) | collective-permute-done | bytes 73760 | tf_op jit(solution)/shard_map/ppermute | solution.py:445
  19.3 0.0 collective-permute-done.1.above
  19.3 0.0 copy-done
  19.3 0.0 copy-done.1
  19.3 1.3 %near.1.known = f32[16,512]{1,0:T(8,128)S(1)} custom-call(s32[3,1,8]{2,1,0:T(1,128)S(1)} %bitcast.5, s32[3,1,14]{2,1,0:T(1,128)S(1)} %bitcast.6, f32[1,16,512]{2,1,0:T(8,128)S(1)} %get-tuple-element.20.charges, bf16[8,192,128]{2,1,0:T(8,128)(2,1)S(1)} %get-tuple-element.25.near_pack, bf16[14,192,128]{2,1,0:T(8,128)(2,1)S(1)} %get-tuple-element.26.coupling_pack, ...), custom_call_target="tpu_custom_call" | custom-call | flops 80000000 | bytes 3000000 | tf_op jit(solution)/shard_map/near/pallas_call | solution.py:484
  20.6 0.0 all-to-all-done
  20.6 1.1 %final.1 = f32[1,16,512]{2,1,0:T(8,128)} custom-call(f32[4,8,8,128]{3,2,1,0:T(8,128)S(1)} %bitcast.4, f32[16,512]{1,0:T(8,128)S(1)} %near.1.known, bf16[2,512,64]{2,1,0:T(8,128)(2,1)S(1)} %get-tuple-element.31.mats, bf16[2,64,512]{2,1,0:T(8,128)(2,1)S(1)} %get-tuple-element.32.path, f32[1,3,2,64,64]{4,3,2,1,0:T(8,128)S(1)} %get-tuple-element.23.coarse_transfer), custom_call_target="tpu_custom_call" | custom-call | flops 10000000 | bytes 600000 | tf_op jit(solution)/shard_map/final/pallas_call | solution.py:511
Async XLA Ops:
  2.6 17.9 %all-to-all-start = ((f32[32,8,128]{2,1,0:T(8,128)}), f32[32,8,128]{2,1,0:T(8,128)S(1)}, u32[]{:S(2)}, u32[]{:S(2)}) async-start(f32[32,8,128]{2,1,0:T(8,128)} %bitcast), calls=%async_computation | async-start | bytes 262144 | tf_op jit(solution)/shard_map/all_to_all | solution.py:447
  10.0 9.3 %collective-permute-start = (f32[9,16,128]{2,1,0:T(8,128)S(1)}, f32[9,16,128]{2,1,0:T(8,128)S(1)}, u32[]{:S(2)}, u32[]{:S(2)}) collective-permute-start(f32[9,16,128]{2,1,0:T(8,128)S(1)} %get-tuple-element.29.mine), channel_id=1, source_target_pairs={{0,4},{4,8},{8,12},{12,16},{16,20},{20,24},{24,28},{28,0},{1,5},{5... | collective-permute-start | bytes 221192 | tf_op jit(solution)/shard_map/ppermute | solution.py:445
  11.8 7.5 %collective-permute-start.1 = (f32[9,16,128]{2,1,0:T(8,128)S(1)}, f32[9,16,128]{2,1,0:T(8,128)S(1)}, u32[]{:S(2)}, u32[]{:S(2)}) collective-permute-start(f32[9,16,128]{2,1,0:T(8,128)S(1)} %get-tuple-element.30), channel_id=1, source_target_pairs={{4,0},{8,4},{12,8},{16,12},{20,16},{24,20},{28,24},{0,28},{5,1},{9... | collective-permute-start | bytes 221192 | tf_op jit(solution)/shard_map/ppermute | solution.py:446
  14.8 4.5 %copy-start = (s32[1,8,3]{1,0,2:T(1,128)S(1)}, s32[1,8,3]{1,0,2:T(1,128)}, u32[]{:S(2)}) copy-start(s32[1,8,3]{1,0,2:T(1,128)} %param.14) | copy-start | bytes 292
  14.8 4.5 %copy-start.1 = (s32[1,14,3]{1,0,2:T(1,128)S(1)}, s32[1,14,3]{1,0,2:T(1,128)}, u32[]{:S(2)}) copy-start(s32[1,14,3]{1,0,2:T(1,128)} %param.17) | copy-start | bytes 508

commit v8 on v7

--- a/solution.py
+++ b/solution.py
@@ -102,6 +102,7 @@
     transfer,
     coarse_transfer,
     coupling,
+    leaf_coeffs,
     sem,
 ):
     copies = fetch(
@@ -128,14 +129,17 @@
         behind[pairs + k] = low
     rhs = charges.shape[1]
     low_lanes = lax.broadcasted_iota(jnp.int32, (rhs, width), 1) < points
-    coeffs = []
-    for j in range(whole):
-        pair = charges[0, :, j * width : (j + 1) * width]
-        left = jnp.concatenate(
-            [jnp.where(low_lanes, pair, 0.0), jnp.where(low_lanes, 0.0, pair)], axis=0
-        )
-        value = mm_s(left, basis[0, 2 * j : 2 * j + 2].reshape(width, basis.shape[3]))
-        coeffs += [value[:rhs], value[rhs:]]
+
+    @pl.when(position >= 0)
+    def _():
+        for j in range(whole):
+            pair = charges[0, :, j * width : (j + 1) * width]
+            left = jnp.concatenate(
+                [jnp.where(low_lanes, pair, 0.0), jnp.where(low_lanes, 0.0, pair)], axis=0
+            )
+            leaf_coeffs[j] = mm_s(left, basis[0, 2 * j : 2 * j + 2].reshape(width, basis.shape[3]))
+
+    coeffs = [leaf_coeffs[g // 2, (g % 2) * rhs : (g % 2 + 1) * rhs] for g in range(leaves)]
     copies[2].wait()
     copies[3].wait()
     tiers = coarse_transfer.shape[1]
@@ -433,7 +437,10 @@
         + like(charges, leaf_basis, local_transfer, coarse_transfer, local_coupling),
         in_specs=[hbm] * 5,
         out_specs=(vmem,) * 8,
-        scratch_shapes=[pltpu.SemaphoreType.DMA((5,))],
+        scratch_shapes=[
+            pltpu.VMEM((leaves // 2, 2 * rhs, rank), f32),
+            pltpu.SemaphoreType.DMA((5,)),
+        ],
         name="up",
         compiler_params=params,
         cost_estimate=pl.CostEstimate(flops=40_000_000, bytes_accessed=1_000_000, transcendentals=0),

time: 21.8 us -> 21.8 us (level)
  no operation moved by 1% of the time
where the time goes in v8:
time: 21.8 us; the launch traced here: 21.6 us
  starting transfers between devices  12.1 us (56%)
  Pallas kernels  6.64 us (30%)
  waiting for transfers between devices  2.82 us (13%)
    all_to_all x1, starting transfers between devices, per_device(): lax.all_to_all(exchange.reshape(leaf_count * top_count, rhs // 2, 2 * ran...  7.33 us
    ppermute x1, starting transfers between devices, per_device(): above = lax.ppermute(behind, 'leaf', backward)  2.95 us
    ppermute x1, waiting for transfers between devices, per_device(): below = lax.ppermute(ahead, 'leaf', forward)  2.82 us
    pallas_call x1, Pallas kernels, per_device(): pl.pallas_call(up_kernel, out_shape=(pack_shape, pack_shape, jax.ShapeDty...  2.64 us
    ppermute x1, starting transfers between devices, per_device(): below = lax.ppermute(ahead, 'leaf', forward)  1.82 us
    pallas_call x1, Pallas kernels, per_device(): pl.pallas_call(prep_kernel, out_shape=(jax.ShapeDtypeStruct((2, rank, lea...  1.7 us
    pallas_call x1, Pallas kernels, per_device(): pl.pallas_call(near_kernel, out_shape=jax.ShapeDtypeStruct((rhs, leaves *...  1.25 us
    pallas_call x1, Pallas kernels, per_device(): pl.pallas_call(final_kernel, out_shape=jax.ShapeDtypeStruct(charges.shape...  1.05 us
  transfers between devices with their start and end apart: 3, of which 1 were waited for; matrix products, arithmetic and copies ran while one was open for 0% of the time, Pallas kernels for 14%

profile of v8, /device:TPU:0, one launch (start us, length us, event | category | flops | bytes accessed | tf_op | source)
XLA Modules:
  0.0 21.6 jit_solution(14520455936383248847)
XLA Ops:
  0.0 2.6 %up.1 = (f32[9,16,128]{2,1,0:T(8,128)S(1)}, f32[9,16,128]{2,1,0:T(8,128)S(1)}, f32[4,8,8,128]{3,2,1,0:T(8,128)}, f32[1,16,512]{2,1,0:T(8,128)S(1)}, f32[1,8,64,6...) custom-call(f32[1,16,512]{2,1,0:T(8,128)} %charges_hbm.1, ...), custom_call_target="tpu_custom_call" | custom-call | flops 40000000 | bytes 1000000 | tf_op jit(solution)/shard_map/up/pallas_call | solution.py:430
  2.6 7.3 %all-to-all-start = ((f32[32,8,128]{2,1,0:T(8,128)}), f32[32,8,128]{2,1,0:T(8,128)S(1)}, u32[]{:S(2)}, u32[]{:S(2)}) async-start(f32[32,8,128]{2,1,0:T(8,128)} %bitcast), calls=%async_computation | async-start | bytes 262144 | tf_op jit(solution)/shard_map/all_to_all | solution.py:454
  10.0 1.8 %collective-permute-start = (f32[9,16,128]{2,1,0:T(8,128)S(1)}, f32[9,16,128]{2,1,0:T(8,128)S(1)}, u32[]{:S(2)}, u32[]{:S(2)}) collective-permute-start(f32[9,16,128]{2,1,0:T(8,128)S(1)} %get-tuple-element.29.mine), channel_id=1, source_target_pairs={{0,4},{4,8},{8,12},{12,16},{16,20},{20,24},{24,28},{28,0},{1,5},{5... | collective-permute-start | bytes 221192 | tf_op jit(solution)/shard_map/ppermute | solution.py:452
  11.8 3.0 %collective-permute-start.1 = (f32[9,16,128]{2,1,0:T(8,128)S(1)}, f32[9,16,128]{2,1,0:T(8,128)S(1)}, u32[]{:S(2)}, u32[]{:S(2)}) collective-permute-start(f32[9,16,128]{2,1,0:T(8,128)S(1)} %get-tuple-element.30), channel_id=1, source_target_pairs={{4,0},{8,4},{12,8},{16,12},{20,16},{24,20},{28,24},{0,28},{5,1},{9... | collective-permute-start | bytes 221192 | tf_op jit(solution)/shard_map/ppermute | solution.py:453
  14.8 0.0 copy-start
  14.8 0.0 copy-start.1
  14.8 1.7 %prep.1 = (bf16[2,64,512]{2,1,0:T(8,128)(2,1)S(1)}, bf16[8,64,128]{2,1,0:T(8,128)(2,1)S(1)}, bf16[4,128,256]{2,1,0:T(8,128)(2,1)S(1)}, bf16[2,512,64]{2,1,0:T(8,...) custom-call(f32[1,8,64,64]{3,2,1,0:T(8,128)S(1)} %get-tuple-element.21.basis, ...), custom_call_target="tpu_custom_call" | custom-call | flops 20000000 | bytes 2000000 | tf_op jit(solution)/shard_map/prep/pallas_call | solution.py:464
  16.5 2.8 %collective-permute-done.below = f32[9,16,128]{2,1,0:T(8,128)S(1)} collective-permute-done((f32[9,16,128]{2,1,0:T(8,128)S(1)}, f32[9,16,128]{2,1,0:T(8,128)S(1)}, u32[]{:S(2)}, u32[]{:S(2)}) %collective-permute-start) | collective-permute-done | bytes 73760 | tf_op jit(solution)/shard_map/ppermute | solution.py:452
  19.3 0.0 collective-permute-done.1.above
  19.3 0.0 copy-done
  19.3 0.0 copy-done.1
  19.3 1.3 %near.1.known = f32[16,512]{1,0:T(8,128)S(1)} custom-call(s32[3,1,8]{2,1,0:T(1,128)S(1)} %bitcast.5, s32[3,1,14]{2,1,0:T(1,128)S(1)} %bitcast.6, f32[1,16,512]{2,1,0:T(8,128)S(1)} %get-tuple-element.20.charges, bf16[8,192,128]{2,1,0:T(8,128)(2,1)S(1)} %get-tuple-element.25.near_pack, bf16[14,192,128]{2,1,0:T(8,128)(2,1)S(1)} %get-tuple-element.26.coupling_pack, ...), custom_call_target="tpu_custom_call" | custom-call | flops 80000000 | bytes 3000000 | tf_op jit(solution)/shard_map/near/pallas_call | solution.py:491
  20.6 0.0 all-to-all-done
  20.6 1.1 %final.1 = f32[1,16,512]{2,1,0:T(8,128)} custom-call(f32[4,8,8,128]{3,2,1,0:T(8,128)S(1)} %bitcast.4, f32[16,512]{1,0:T(8,128)S(1)} %near.1.known, bf16[2,512,64]{2,1,0:T(8,128)(2,1)S(1)} %get-tuple-element.31.mats, bf16[2,64,512]{2,1,0:T(8,128)(2,1)S(1)} %get-tuple-element.32.path, f32[1,3,2,64,64]{4,3,2,1,0:T(8,128)S(1)} %get-tuple-element.23.coarse_transfer), custom_call_target="tpu_custom_call" | custom-call | flops 10000000 | bytes 600000 | tf_op jit(solution)/shard_map/final/pallas_call | solution.py:518
Async XLA Ops:
  2.6 17.9 %all-to-all-start = ((f32[32,8,128]{2,1,0:T(8,128)}), f32[32,8,128]{2,1,0:T(8,128)S(1)}, u32[]{:S(2)}, u32[]{:S(2)}) async-start(f32[32,8,128]{2,1,0:T(8,128)} %bitcast), calls=%async_computation | async-start | bytes 262144 | tf_op jit(solution)/shard_map/all_to_all | solution.py:454
  10.0 9.3 %collective-permute-start = (f32[9,16,128]{2,1,0:T(8,128)S(1)}, f32[9,16,128]{2,1,0:T(8,128)S(1)}, u32[]{:S(2)}, u32[]{:S(2)}) collective-permute-start(f32[9,16,128]{2,1,0:T(8,128)S(1)} %get-tuple-element.29.mine), channel_id=1, source_target_pairs={{0,4},{4,8},{8,12},{12,16},{16,20},{20,24},{24,28},{28,0},{1,5},{5... | collective-permute-start | bytes 221192 | tf_op jit(solution)/shard_map/ppermute | solution.py:452
  11.8 7.5 %collective-permute-start.1 = (f32[9,16,128]{2,1,0:T(8,128)S(1)}, f32[9,16,128]{2,1,0:T(8,128)S(1)}, u32[]{:S(2)}, u32[]{:S(2)}) collective-permute-start(f32[9,16,128]{2,1,0:T(8,128)S(1)} %get-tuple-element.30), channel_id=1, source_target_pairs={{4,0},{8,4},{12,8},{16,12},{20,16},{24,20},{28,24},{0,28},{5,1},{9... | collective-permute-start | bytes 221192 | tf_op jit(solution)/shard_map/ppermute | solution.py:453
  14.8 4.5 %copy-start = (s32[1,8,3]{1,0,2:T(1,128)S(1)}, s32[1,8,3]{1,0,2:T(1,128)}, u32[]{:S(2)}) copy-start(s32[1,8,3]{1,0,2:T(1,128)} %param.14) | copy-start | bytes 292
  14.8 4.5 %copy-start.1 = (s32[1,14,3]{1,0,2:T(1,128)S(1)}, s32[1,14,3]{1,0,2:T(1,128)}, u32[]{:S(2)}) copy-start(s32[1,14,3]{1,0,2:T(1,128)} %param.17) | copy-start | bytes 508
